TPU v7x, 256 devices: a whole 4x4x8 slice. The times are simulated.
256 devices in a mesh: gx: 4 (over x), gy: 8 (over y, core), ha: 8 (over z).
Axes of the slice: x: 4, y: 4, z: 8, core: 2. Of those that a mesh axis runs over, the one named last changes fastest.
Arguments:
- level_set: float32 [32, 128, 80, 128], P('gx', 'gy', 'ha'), may hold values from -4 to 4
- wind_field: float32 [2, 32, 128], P(None, 'gx', 'gy'), may hold values from -3 to 3
Outputs:
- increment: float32 [32, 128, 80, 128], P('gx', 'gy', 'ha')
All inputs are finite; a program needn't handle non-finite values.
Results may differ from a plain program's by a relative error of at most 0.000073.
Values sent between devices are 32-bit elements; how exact they have to be, the bound alone decides.
A program may use at most 128 MiB of HBM per device.

v0:
```python
import math

import jax
import jax.numpy as jnp
from jax import lax
from jax.sharding import PartitionSpec as P

CELL_SIZE = 0.05
SPEED_LOW = 0.1
SPEED_SPAN = 0.4
TURN_MAX = 1.0
ACCEL_MAX = 0.05
CFL_NUMBER = 0.5
WENO_EPS = 1e-06


def from_everyone(value, axis):
    copies = jnp.broadcast_to(value, (lax.axis_size(axis), *value.shape))
    return lax.all_to_all(copies, axis, split_axis=0, concat_axis=0, tiled=True)


def over_copies(value, axis):
    everything = from_everyone(value, axis)
    return jnp.max(everything, axis=0)


def extended_2(value, sides, width):
    edges = {}
    for axis, dim in sides:
        size, length = (lax.axis_size(axis), value.shape[dim])
        up = [(i, (i + 1) % size) for i in range(size - 1)]
        last = lax.slice_in_dim(value, length - width, length, axis=dim)
        initial = lax.slice_in_dim(value, 0, width, axis=dim)
        edges[dim] = (
            lax.ppermute(last, axis, up),
            lax.ppermute(initial, axis, [(b, a) for a, b in up]),
        )
    done = []
    for _, dim in sides:
        low, high = edges[dim]
        around = [(width, width) if d in done else (0, 0) for d in range(value.ndim)]
        value = jnp.concatenate([jnp.pad(low, around), value, jnp.pad(high, around)], axis=dim)
        done.append(dim)
    return value


def with_halo(cells, sides, width):
    for axis, dim in sides:
        count = lax.axis_size(axis)
        head = lax.slice_in_dim(cells, 0, width, axis=dim)
        tail = lax.slice_in_dim(cells, cells.shape[dim] - width, cells.shape[dim], axis=dim)
        cells = jnp.concatenate(
            [
                lax.ppermute(tail, axis, [(i, (i + 1) % count) for i in range(count)]),
                cells,
                lax.ppermute(head, axis, [((i + 1) % count, i) for i in range(count)]),
            ],
            axis=dim,
        )
    return cells


def ghost_rows(values, along, at_low):
    length = values.shape[along]
    if at_low:
        edge_row = lax.slice_in_dim(values, 0, 1, axis=along)
        next_row = lax.slice_in_dim(values, 1, 2, axis=along)
        reaches = (3.0, 2.0, 1.0)
    else:
        edge_row = lax.slice_in_dim(values, length - 1, length, axis=along)
        next_row = lax.slice_in_dim(values, length - 2, length - 1, axis=along)
        reaches = (1.0, 2.0, 3.0)
    slope_edge = edge_row - next_row
    return jnp.concatenate([edge_row + distance * slope_edge for distance in reaches], axis=along)


def fix_edges(extended, along, at_start, at_end, length):
    interior = lax.slice_in_dim(extended, 3, 3 + length, axis=along)
    below_rows = jnp.where(
        at_start, ghost_rows(interior, along, True), lax.slice_in_dim(extended, 0, 3, axis=along)
    )
    above_rows = jnp.where(
        at_end,
        ghost_rows(interior, along, False),
        lax.slice_in_dim(extended, 3 + length, 6 + length, axis=along),
    )
    return jnp.concatenate([below_rows, interior, above_rows], axis=along)


def speed_shifts(values):
    length = values.shape[3]
    below_rows = ghost_rows(values, 3, True)
    above_rows = ghost_rows(values, 3, False)
    shifted = []
    for displace in range(-3, 4):
        pieces = []
        if displace < 0:
            pieces.append(lax.slice_in_dim(below_rows, 3 + displace, 3, axis=3))
        pieces.append(lax.slice_in_dim(values, max(displace, 0), length + min(displace, 0), axis=3))
        if displace > 0:
            pieces.append(lax.slice_in_dim(above_rows, 0, displace, axis=3))
        shifted.append(jnp.concatenate(pieces, axis=3) if len(pieces) > 1 else pieces[0])
    return shifted


def weno_side(left_far, left_near, middle, right_near, right_far):
    guess_one = left_far * (1.0 / 3.0) - left_near * (7.0 / 6.0) + middle * (11.0 / 6.0)
    guess_two = -left_near * (1.0 / 6.0) + middle * (5.0 / 6.0) + right_near * (1.0 / 3.0)
    guess_three = middle * (1.0 / 3.0) + right_near * (5.0 / 6.0) - right_far * (1.0 / 6.0)
    smooth_one = 13.0 / 12.0 * jnp.square(left_far - 2.0 * left_near + middle) + 0.25 * jnp.square(
        left_far - 4.0 * left_near + 3.0 * middle
    )
    smooth_two = 13.0 / 12.0 * jnp.square(
        left_near - 2.0 * middle + right_near
    ) + 0.25 * jnp.square(left_near - right_near)
    smooth_three = 13.0 / 12.0 * jnp.square(
        middle - 2.0 * right_near + right_far
    ) + 0.25 * jnp.square(3.0 * middle - 4.0 * right_near + right_far)
    weight_one = 0.1 / jnp.square(smooth_one + WENO_EPS)
    weight_two = 0.6 / jnp.square(smooth_two + WENO_EPS)
    weight_three = 0.3 / jnp.square(smooth_three + WENO_EPS)
    return (weight_one * guess_one + weight_two * guess_two + weight_three * guess_three) / (
        weight_one + weight_two + weight_three
    )


def weno_pair(shifted, spacing):
    slopes = [(shifted[position + 1] - shifted[position]) / spacing for position in range(6)]
    left_slope = weno_side(slopes[0], slopes[1], slopes[2], slopes[3], slopes[4])
    right_slope = weno_side(slopes[5], slopes[4], slopes[3], slopes[2], slopes[1])
    return (left_slope, right_slope)


def cell_rates(cos_head, sin_head, speeds, wind_x, wind_y, d_theta, d_speed):
    along_x = speeds[None, None, None, :] * cos_head[None, None, :, None] + wind_x[:, :, None, None]
    along_y = speeds[None, None, None, :] * sin_head[None, None, :, None] + wind_y[:, :, None, None]
    return (
        jnp.abs(along_x) / CELL_SIZE
        + jnp.abs(along_y) / CELL_SIZE
        + TURN_MAX / d_theta
        + ACCEL_MAX / d_speed
    )


def hamilton(x_pair, y_pair, head_pair, speed_pair, cos_head, sin_head, speeds, wind_x, wind_y):
    flow_x = speeds[None, None, None, :] * cos_head[None, None, :, None] + wind_x[:, :, None, None]
    flow_y = speeds[None, None, None, :] * sin_head[None, None, :, None] + wind_y[:, :, None, None]
    mean_x = 0.5 * (x_pair[0] + x_pair[1])
    mean_y = 0.5 * (y_pair[0] + y_pair[1])
    mean_head = 0.5 * (head_pair[0] + head_pair[1])
    mean_speed = 0.5 * (speed_pair[0] + speed_pair[1])
    value = -(
        flow_x * mean_x
        + flow_y * mean_y
        + TURN_MAX * jnp.abs(mean_head)
        + ACCEL_MAX * jnp.abs(mean_speed)
    )
    damping = 0.5 * (
        jnp.abs(flow_x) * (x_pair[1] - x_pair[0])
        + jnp.abs(flow_y) * (y_pair[1] - y_pair[0])
        + TURN_MAX * (head_pair[1] - head_pair[0])
        + ACCEL_MAX * (speed_pair[1] - speed_pair[0])
    )
    return -jnp.maximum(value - damping, 0.0)


def body(level_set, wind_field):
    cells_x, cells_y, cells_h, cells_v = level_set.shape
    n_head = cells_h * lax.axis_size("ha")
    head_base = lax.axis_index("ha") * cells_h
    start_x = lax.axis_index("gx") == 0
    end_x = lax.axis_index("gx") == lax.axis_size("gx") - 1
    start_y = lax.axis_index("gy") == 0
    end_y = lax.axis_index("gy") == lax.axis_size("gy") - 1
    wind_x = wind_field[0]
    wind_y = wind_field[1]
    d_theta = 2.0 * math.pi / n_head
    d_speed = SPEED_SPAN / cells_v
    speeds = (
        SPEED_LOW
        + SPEED_SPAN * (jnp.arange(cells_v, dtype=jnp.int32).astype(jnp.float32) + 0.5) / cells_v
    )

    def headings(offset, height):
        slots = (head_base - offset + jnp.arange(height, dtype=jnp.int32) + n_head) % n_head
        angles = slots.astype(jnp.float32) * d_theta
        return (jnp.cos(angles), jnp.sin(angles))

    every_angle = jnp.arange(n_head, dtype=jnp.int32).astype(jnp.float32) * d_theta
    end_speeds = jnp.stack([speeds[0], speeds[cells_v - 1]])
    local_top = jnp.max(
        cell_rates(
            jnp.cos(every_angle), jnp.sin(every_angle), end_speeds, wind_x, wind_y, d_theta, d_speed
        )
    )
    top_rate = over_copies(local_top, ("gx", "gy"))
    time_step = CFL_NUMBER / top_rate

    def slope_field(center, around, offset):
        height = center.shape[2]
        extended = extended_2(center, (("gx", 0), ("gy", 1)), 3)
        extended = fix_edges(extended, 0, start_x, end_x, cells_x)
        extended = fix_edges(extended, 1, start_y, end_y, cells_y)
        x_shifted = [
            extended[3 + displace : 3 + displace + cells_x, 3 : 3 + cells_y]
            for displace in range(-3, 4)
        ]
        y_shifted = [
            extended[3 : 3 + cells_x, 3 + displace : 3 + displace + cells_y]
            for displace in range(-3, 4)
        ]
        head_shifted = [
            around[:, :, 3 + displace : 3 + displace + height] for displace in range(-3, 4)
        ]
        cos_head, sin_head = headings(offset, height)
        return hamilton(
            weno_pair(x_shifted, CELL_SIZE),
            weno_pair(y_shifted, CELL_SIZE),
            weno_pair(head_shifted, d_theta),
            weno_pair(speed_shifts(center), d_speed),
            cos_head,
            sin_head,
            speeds,
            wind_x,
            wind_y,
        )

    def around_heads(surface):
        return with_halo(surface, (("ha", 2),), 3)

    section_one = level_set + time_step * slope_field(level_set, around_heads(level_set), 0)
    section_two = 0.75 * level_set + 0.25 * (
        section_one + time_step * slope_field(section_one, around_heads(section_one), 0)
    )
    advanced = 1.0 / 3.0 * level_set + 2.0 / 3.0 * (
        section_two + time_step * slope_field(section_two, around_heads(section_two), 0)
    )
    return advanced - level_set


def solution(mesh):
    return jax.shard_map(
        body,
        mesh=mesh,
        in_specs=(P("gx", "gy", "ha", None), P(None, "gx", "gy")),
        out_specs=P("gx", "gy", "ha", None),
        check_vma=False,
    )
```

profile of v0, /device:TPU:1, one launch (start us, length us, event | category | flops | bytes accessed | tf_op | source)
XLA Modules:
  0.0 152.8 jit_solution(8316435247508885770)
XLA Ops:
  0.0 1.5 %copy.129 = f32[8,16,10,128]{3,0,2,1:T(8,128)S(1)} copy(f32[8,16,10,128]{3,1,2,0:T(8,128)} %param.2) | data formatting | bytes 1310720 | tf_op args[0]
  2.3 4.6 %collective-permute-start = (f32[8,3,10,128]{3,0,2,1:T(8,128)}, f32[8,3,10,128]{3,0,2,1:T(8,128)}, u32[]{:S(2)}, u32[]{:S(2)}) collective-permute-start(f32[8,3,10,128]{3,0,2,1:T(8,128)} %get-tuple-element.127), channel_id=1, source_target_pairs={{0,8},{8,16},{16,24},{24,32},{32,40},{40,48},{48,56},{1,9},{9,17},... | collective-permute-start | bytes 368648 | tf_op jit(solution)/shard_map/ppermute | solution.py:35
  6.8 2.4 %collective-permute-start.3 = (f32[8,3,10,128]{3,0,2,1:T(8,128)}, f32[8,3,10,128]{3,0,2,1:T(8,128)}, u32[]{:S(2)}, u32[]{:S(2)}) collective-permute-start(f32[8,3,10,128]{3,0,2,1:T(8,128)} %get-tuple-element.128), channel_id=1, source_target_pairs={{8,0},{16,8},{24,16},{32,24},{40,32},{48,40},{56,48},{9,1},{17,9},... | collective-permute-start | bytes 368648 | tf_op jit(solution)/shard_map/ppermute | solution.py:36
  10.1 3.3 %collective-permute-start.1 = (f32[3,16,10,128]{3,1,2,0:T(8,128)}, f32[3,16,10,128]{3,1,2,0:T(8,128)}, u32[]{:S(2)}, u32[]{:S(2)}) collective-permute-start(f32[3,16,10,128]{3,1,2,0:T(8,128)} %get-tuple-element.125), channel_id=1, source_target_pairs={{0,64},{64,128},{128,192},{1,65},{65,129},{129,193},{2,66},{66,130... | collective-permute-start | bytes 737288 | tf_op jit(solution)/shard_map/ppermute | solution.py:35
  15.9 1.3 pad_maximum_fusion.37
  19.3 8.4 %all-to-all-start = ((f32[32,1,1]{2,1,0:T(1,128)}), f32[32,1,1]{2,1,0:T(1,128)}, u32[]{:S(2)}, u32[]{:S(2)}) async-start(f32[32,1,1]{2,1,0:T(1,128)} %broadcast_in_dim.2), calls=%async_computation | async-start | bytes 32768 | tf_op jit(solution)/shard_map/all_to_all | solution.py:19
  28.5 1.6 %collective-permute-start.4 = (f32[8,16,3,128]{3,0,2,1:T(8,128)}, f32[8,16,3,128]{3,0,2,1:T(8,128)}, u32[]{:S(2)}, u32[]{:S(2)}) collective-permute-start(f32[8,16,3,128]{3,0,2,1:T(8,128)} %get-tuple-element.131), channel_id=1, source_target_pairs={{0,1},{1,2},{2,3},{3,4},{4,5},{5,6},{6,7},{7,0},{8,9},{9,10},{10,1... | collective-permute-start | bytes 589832 | tf_op jit(solution)/shard_map/ppermute | solution.py:54
  30.1 1.8 %multiply_add_fusion.28 = (f32[8,16,10,1]{3,0,2,1:T(8,128)S(1)}, f32[8,16,10,1]{3,0,2,1:T(8,128)S(1)}, f32[8,16,10,1]{3,0,2,1:T(8,128)S(1)}, f32[8,16,10,1]{3,0,...) fusion(f32[8,16,10,128]{3,0,2,1:T(8,128)S(1)} %copy.129), kind=kLoop, calls=%fused_computation.663 | loop fusion | flops 15360 | bytes 51200 | tf_op jit(solution)/shard_map/add | solution.py:74
  36.6 1.4 reduce_max.19
  39.3 3.4 %collective-permute-start.5 = (f32[8,16,3,128]{3,0,2,1:T(8,128)}, f32[8,16,3,128]{3,0,2,1:T(8,128)S(1)}, u32[]{:S(2)}, u32[]{:S(2)}) collective-permute-start(f32[8,16,3,128]{3,0,2,1:T(8,128)} %get-tuple-element.132), channel_id=1, source_target_pairs={{1,0},{2,1},{3,2},{4,3},{5,4},{6,5},{7,6},{0,7},{9,8},{10,9},{11,1... | collective-permute-start | bytes 589832 | tf_op jit(solution)/shard_map/ppermute | solution.py:56
  44.1 2.9 %collective-permute-done.5 = f32[8,16,3,128]{3,0,2,1:T(8,128)S(1)} collective-permute-done((f32[8,16,3,128]{3,0,2,1:T(8,128)}, f32[8,16,3,128]{3,0,2,1:T(8,128)S(1)}, u32[]{:S(2)}, u32[]{:S(2)}) %collective-permute-start.5) | collective-permute-done | bytes 196640 | tf_op jit(solution)/shard_map/ppermute | solution.py:56
  54.6 18.9 %fusion.24 = f32[8,16,10,128]{3,0,2,1:T(8,128)S(1)} fusion(f32[8,16,10,1]{3,0,2,1:T(8,128)S(1)} %copy-done.3, f32[8,16,10,1]{3,0,2,1:T(8,128)S(1)} %copy-done.1, f32[8,16,10,1]{3,0,2,1:T(8,128)S(1)} %copy-done.2, f32[8,16,10,125]{3,0,2,1:T(8,128)S(1)} %copy-done.9, f32[8,16,10,126]{3,0,2,1:T(8,128)S(1)} %copy-done.7, f32[8,16,10,127]{3,0,2,1:T(8,128)S(1)} %copy-done.5, ...), kind=kLoop, calls=%fused_computation.107 | loop fusion | flops 99123200 | bytes 12309508 | tf_op jit(solution)/shard_map/add | solution.py:231
  75.0 3.2 %collective-permute-start.7 = (f32[3,16,10,128]{3,1,2,0:T(8,128)S(1)}, f32[3,16,10,128]{3,1,2,0:T(8,128)S(1)}, u32[]{:S(2)}, u32[]{:S(2)}) collective-permute-start(f32[3,16,10,128]{3,1,2,0:T(8,128)S(1)} %copy.162), channel_id=1, source_target_pairs={{0,64},{64,128},{128,192},{1,65},{65,129},{129,193},{2,66},{66,130... | collective-permute-start | bytes 737288 | tf_op jit(solution)/shard_map/ppermute | solution.py:35
  78.2 1.3 collective-permute-start.8
  79.5 4.7 %collective-permute-start.6 = (f32[8,3,10,128]{3,0,2,1:T(8,128)S(1)}, f32[8,3,10,128]{3,0,2,1:T(8,128)S(1)}, u32[]{:S(2)}, u32[]{:S(2)}) collective-permute-start(f32[8,3,10,128]{3,0,2,1:T(8,128)S(1)} %get-tuple-element.109), channel_id=1, source_target_pairs={{0,8},{8,16},{16,24},{24,32},{32,40},{40,48},{48,56},{1,9},{9,17},... | collective-permute-start | bytes 368648 | tf_op jit(solution)/shard_map/ppermute | solution.py:35
  84.2 1.9 %collective-permute-start.9 = (f32[8,3,10,128]{3,0,2,1:T(8,128)S(1)}, f32[8,3,10,128]{3,0,2,1:T(8,128)S(1)}, u32[]{:S(2)}, u32[]{:S(2)}) collective-permute-start(f32[8,3,10,128]{3,0,2,1:T(8,128)S(1)} %get-tuple-element.110), channel_id=1, source_target_pairs={{8,0},{16,8},{24,16},{32,24},{40,32},{48,40},{56,48},{9,1},{17,9},... | collective-permute-start | bytes 368648 | tf_op jit(solution)/shard_map/ppermute | solution.py:36
  86.3 3.4 %collective-permute-start.11 = (f32[8,16,3,128]{3,0,2,1:T(8,128)S(1)}, f32[8,16,3,128]{3,0,2,1:T(8,128)S(1)}, u32[]{:S(2)}, u32[]{:S(2)}) collective-permute-start(f32[8,16,3,128]{3,0,2,1:T(8,128)S(1)} %get-tuple-element.112), channel_id=1, source_target_pairs={{1,0},{2,1},{3,2},{4,3},{5,4},{6,5},{7,6},{0,7},{9,8},{10,9},{11,1... | collective-permute-start | bytes 589832 | tf_op jit(solution)/shard_map/ppermute | solution.py:56
  93.6 18.4 %fusion.35 = f32[8,16,10,128]{3,0,2,1:T(8,128)S(1)} fusion(f32[8,16,10,128]{3,0,2,1:T(8,128)S(1)} %fusion.24, f32[8,16,10,1]{3,0,2,1:T(8,128)S(1)} %get-tuple-element.119, f32[8,16,10,1]{3,0,2,1:T(8,128)S(1)} %get-tuple-element.118, f32[8,16,10,1]{3,0,2,1:T(8,128)S(1)} %get-tuple-element.122, f32[8,16,10,125]{3,0,2,1:T(8,128)S(1)} %get-tuple-element.124, ...), kind=kLoop, calls=%fused_computation.118 | loop fusion | flops 100597760 | bytes 9425924 | tf_op jit(solution)/shard_map/add | solution.py:232
  113.5 4.3 %collective-permute-start.13 = (f32[3,16,10,128]{3,1,2,0:T(8,128)S(1)}, f32[3,16,10,128]{3,1,2,0:T(8,128)S(1)}, u32[]{:S(2)}, u32[]{:S(2)}) collective-permute-start(f32[3,16,10,128]{3,1,2,0:T(8,128)S(1)} %copy.166), channel_id=1, source_target_pairs={{0,64},{64,128},{128,192},{1,65},{65,129},{129,193},{2,66},{66,130... | collective-permute-start | bytes 737288 | tf_op jit(solution)/shard_map/ppermute | solution.py:35
  117.8 1.3 collective-permute-start.14
  119.2 5.0 %collective-permute-start.12 = (f32[8,3,10,128]{3,0,2,1:T(8,128)S(1)}, f32[8,3,10,128]{3,0,2,1:T(8,128)S(1)}, u32[]{:S(2)}, u32[]{:S(2)}) collective-permute-start(f32[8,3,10,128]{3,0,2,1:T(8,128)S(1)} %get-tuple-element.91), channel_id=1, source_target_pairs={{0,8},{8,16},{16,24},{24,32},{32,40},{40,48},{48,56},{1,9},{9,17},... | collective-permute-start | bytes 368648 | tf_op jit(solution)/shard_map/ppermute | solution.py:35
  124.2 1.9 %collective-permute-start.15 = (f32[8,3,10,128]{3,0,2,1:T(8,128)S(1)}, f32[8,3,10,128]{3,0,2,1:T(8,128)S(1)}, u32[]{:S(2)}, u32[]{:S(2)}) collective-permute-start(f32[8,3,10,128]{3,0,2,1:T(8,128)S(1)} %get-tuple-element.92), channel_id=1, source_target_pairs={{8,0},{16,8},{24,16},{32,24},{40,32},{48,40},{56,48},{9,1},{17,9},... | collective-permute-start | bytes 368648 | tf_op jit(solution)/shard_map/ppermute | solution.py:36
  126.2 2.3 %collective-permute-start.16 = (f32[8,16,3,128]{3,0,2,1:T(8,128)S(1)}, f32[8,16,3,128]{3,0,2,1:T(8,128)S(1)}, u32[]{:S(2)}, u32[]{:S(2)}) collective-permute-start(f32[8,16,3,128]{3,0,2,1:T(8,128)S(1)} %get-tuple-element.93), channel_id=1, source_target_pairs={{0,1},{1,2},{2,3},{3,4},{4,5},{5,6},{6,7},{7,0},{8,9},{9,10},{10,1... | collective-permute-start | bytes 589832 | tf_op jit(solution)/shard_map/ppermute | solution.py:54
  133.3 18.5 %fusion.47 = f32[8,16,10,128]{3,0,2,1:T(8,128)S(1)} fusion(f32[8,16,10,128]{3,0,2,1:T(8,128)S(1)} %fusion.35, f32[8,16,10,1]{3,0,2,1:T(8,128)S(1)} %get-tuple-element.101, f32[8,16,10,1]{3,0,2,1:T(8,128)S(1)} %get-tuple-element.100, f32[8,16,10,1]{3,0,2,1:T(8,128)S(1)} %get-tuple-element.104, f32[8,16,10,125]{3,0,2,1:T(8,128)S(1)} %get-tuple-element.106, ...), kind=kLoop, calls=%fused_computation.130 | loop fusion | flops 100761600 | bytes 9425924 | tf_op jit(solution)/shard_map/sub | solution.py:238
  (117 shorter events, 33.6 us)
Async XLA Ops:
  0.0 9.3 %copy-start = (f32[8,16,10,128]{3,1,2,0:T(8,128)S(1)}, f32[8,16,10,128]{3,1,2,0:T(8,128)}, u32[]{:S(2)}) copy-start(f32[8,16,10,128]{3,1,2,0:T(8,128)} %param.2) | copy-start | bytes 1966084
  0.0 15.9 %copy-start.10 = (f32[2,8,16]{2,1,0:T(8,128)S(1)}, f32[2,8,16]{2,1,0:T(8,128)}, u32[]{:S(2)}) copy-start(f32[2,8,16]{2,1,0:T(8,128)} %param.3) | copy-start | bytes 3076
  2.3 46.1 %collective-permute-start = (f32[8,3,10,128]{3,0,2,1:T(8,128)}, f32[8,3,10,128]{3,0,2,1:T(8,128)}, u32[]{:S(2)}, u32[]{:S(2)}) collective-permute-start(f32[8,3,10,128]{3,0,2,1:T(8,128)} %get-tuple-element.127), channel_id=1, source_target_pairs={{0,8},{8,16},{16,24},{24,32},{32,40},{40,48},{48,56},{1,9},{9,17},... | collective-permute-start | bytes 368648 | tf_op jit(solution)/shard_map/ppermute | solution.py:35
  6.8 41.5 %collective-permute-start.3 = (f32[8,3,10,128]{3,0,2,1:T(8,128)}, f32[8,3,10,128]{3,0,2,1:T(8,128)}, u32[]{:S(2)}, u32[]{:S(2)}) collective-permute-start(f32[8,3,10,128]{3,0,2,1:T(8,128)} %get-tuple-element.128), channel_id=1, source_target_pairs={{8,0},{16,8},{24,16},{32,24},{40,32},{48,40},{56,48},{9,1},{17,9},... | collective-permute-start | bytes 368648 | tf_op jit(solution)/shard_map/ppermute | solution.py:36
  10.1 36.9 %collective-permute-start.1 = (f32[3,16,10,128]{3,1,2,0:T(8,128)}, f32[3,16,10,128]{3,1,2,0:T(8,128)}, u32[]{:S(2)}, u32[]{:S(2)}) collective-permute-start(f32[3,16,10,128]{3,1,2,0:T(8,128)} %get-tuple-element.125), channel_id=1, source_target_pairs={{0,64},{64,128},{128,192},{1,65},{65,129},{129,193},{2,66},{66,130... | collective-permute-start | bytes 737288 | tf_op jit(solution)/shard_map/ppermute | solution.py:35
  13.4 34.7 %collective-permute-start.2 = (f32[3,16,10,128]{3,1,2,0:T(8,128)}, f32[3,16,10,128]{3,1,2,0:T(8,128)S(1)}, u32[]{:S(2)}, u32[]{:S(2)}) collective-permute-start(f32[3,16,10,128]{3,1,2,0:T(8,128)} %get-tuple-element.126), channel_id=1, source_target_pairs={{64,0},{128,64},{192,128},{65,1},{129,65},{193,129},{66,2},{130,66... | collective-permute-start | bytes 737288 | tf_op jit(solution)/shard_map/ppermute | solution.py:36
  19.3 17.4 %all-to-all-start = ((f32[32,1,1]{2,1,0:T(1,128)}), f32[32,1,1]{2,1,0:T(1,128)}, u32[]{:S(2)}, u32[]{:S(2)}) async-start(f32[32,1,1]{2,1,0:T(1,128)} %broadcast_in_dim.2), calls=%async_computation | async-start | bytes 32768 | tf_op jit(solution)/shard_map/all_to_all | solution.py:19
  28.5 10.9 %collective-permute-start.4 = (f32[8,16,3,128]{3,0,2,1:T(8,128)}, f32[8,16,3,128]{3,0,2,1:T(8,128)}, u32[]{:S(2)}, u32[]{:S(2)}) collective-permute-start(f32[8,16,3,128]{3,0,2,1:T(8,128)} %get-tuple-element.131), channel_id=1, source_target_pairs={{0,1},{1,2},{2,3},{3,4},{4,5},{5,6},{6,7},{7,0},{8,9},{9,10},{10,1... | collective-permute-start | bytes 589832 | tf_op jit(solution)/shard_map/ppermute | solution.py:54
  39.3 7.6 %collective-permute-start.5 = (f32[8,16,3,128]{3,0,2,1:T(8,128)}, f32[8,16,3,128]{3,0,2,1:T(8,128)S(1)}, u32[]{:S(2)}, u32[]{:S(2)}) collective-permute-start(f32[8,16,3,128]{3,0,2,1:T(8,128)} %get-tuple-element.132), channel_id=1, source_target_pairs={{1,0},{2,1},{3,2},{4,3},{5,4},{6,5},{7,6},{0,7},{9,8},{10,9},{11,1... | collective-permute-start | bytes 589832 | tf_op jit(solution)/shard_map/ppermute | solution.py:56
  52.0 2.2 %copy-start.4 = (f32[8,16,10,127]{3,0,2,1:T(8,128)S(1)}, f32[8,16,10,127]{3,0,2,1:T(8,128)}, u32[]{:S(2)}) copy-start(f32[8,16,10,127]{3,0,2,1:T(8,128)} %get-tuple-element.133) | copy-start | bytes 1950724
  52.0 2.4 %copy-start.5 = (f32[8,16,10,127]{3,0,2,1:T(8,128)S(1)}, f32[8,16,10,127]{3,0,2,1:T(8,128)}, u32[]{:S(2)}) copy-start(f32[8,16,10,127]{3,0,2,1:T(8,128)} %get-tuple-element.134) | copy-start | bytes 1950724
  52.0 2.5 %copy-start.6 = (f32[8,16,10,126]{3,0,2,1:T(8,128)S(1)}, f32[8,16,10,126]{3,0,2,1:T(8,128)}, u32[]{:S(2)}) copy-start(f32[8,16,10,126]{3,0,2,1:T(8,128)} %get-tuple-element.135) | copy-start | bytes 1935364
  75.0 11.3 %collective-permute-start.7 = (f32[3,16,10,128]{3,1,2,0:T(8,128)S(1)}, f32[3,16,10,128]{3,1,2,0:T(8,128)S(1)}, u32[]{:S(2)}, u32[]{:S(2)}) collective-permute-start(f32[3,16,10,128]{3,1,2,0:T(8,128)S(1)} %copy.162), channel_id=1, source_target_pairs={{0,64},{64,128},{128,192},{1,65},{65,129},{129,193},{2,66},{66,130... | collective-permute-start | bytes 737288 | tf_op jit(solution)/shard_map/ppermute | solution.py:35
  78.2 11.6 %collective-permute-start.8 = (f32[3,16,10,128]{3,1,2,0:T(8,128)S(1)}, f32[3,16,10,128]{3,1,2,0:T(8,128)S(1)}, u32[]{:S(2)}, u32[]{:S(2)}) collective-permute-start(f32[3,16,10,128]{3,1,2,0:T(8,128)S(1)} %copy.163), channel_id=1, source_target_pairs={{64,0},{128,64},{192,128},{65,1},{129,65},{193,129},{66,2},{130,66... | collective-permute-start | bytes 737288 | tf_op jit(solution)/shard_map/ppermute | solution.py:36
  79.5 10.5 %collective-permute-start.6 = (f32[8,3,10,128]{3,0,2,1:T(8,128)S(1)}, f32[8,3,10,128]{3,0,2,1:T(8,128)S(1)}, u32[]{:S(2)}, u32[]{:S(2)}) collective-permute-start(f32[8,3,10,128]{3,0,2,1:T(8,128)S(1)} %get-tuple-element.109), channel_id=1, source_target_pairs={{0,8},{8,16},{16,24},{24,32},{32,40},{40,48},{48,56},{1,9},{9,17},... | collective-permute-start | bytes 368648 | tf_op jit(solution)/shard_map/ppermute | solution.py:35
  84.2 6.5 %collective-permute-start.9 = (f32[8,3,10,128]{3,0,2,1:T(8,128)S(1)}, f32[8,3,10,128]{3,0,2,1:T(8,128)S(1)}, u32[]{:S(2)}, u32[]{:S(2)}) collective-permute-start(f32[8,3,10,128]{3,0,2,1:T(8,128)S(1)} %get-tuple-element.110), channel_id=1, source_target_pairs={{8,0},{16,8},{24,16},{32,24},{40,32},{48,40},{56,48},{9,1},{17,9},... | collective-permute-start | bytes 368648 | tf_op jit(solution)/shard_map/ppermute | solution.py:36
  86.2 7.4 %collective-permute-start.10 = (f32[8,16,3,128]{3,0,2,1:T(8,128)S(1)}, f32[8,16,3,128]{3,0,2,1:T(8,128)S(1)}, u32[]{:S(2)}, u32[]{:S(2)}) collective-permute-start(f32[8,16,3,128]{3,0,2,1:T(8,128)S(1)} %get-tuple-element.111), channel_id=1, source_target_pairs={{0,1},{1,2},{2,3},{3,4},{4,5},{5,6},{6,7},{7,0},{8,9},{9,10},{10,1... | collective-permute-start | bytes 589832 | tf_op jit(solution)/shard_map/ppermute | solution.py:54
  86.3 7.3 %collective-permute-start.11 = (f32[8,16,3,128]{3,0,2,1:T(8,128)S(1)}, f32[8,16,3,128]{3,0,2,1:T(8,128)S(1)}, u32[]{:S(2)}, u32[]{:S(2)}) collective-permute-start(f32[8,16,3,128]{3,0,2,1:T(8,128)S(1)} %get-tuple-element.112), channel_id=1, source_target_pairs={{1,0},{2,1},{3,2},{4,3},{5,4},{6,5},{7,6},{0,7},{9,8},{10,9},{11,1... | collective-permute-start | bytes 589832 | tf_op jit(solution)/shard_map/ppermute | solution.py:56
  113.5 14.9 %collective-permute-start.13 = (f32[3,16,10,128]{3,1,2,0:T(8,128)S(1)}, f32[3,16,10,128]{3,1,2,0:T(8,128)S(1)}, u32[]{:S(2)}, u32[]{:S(2)}) collective-permute-start(f32[3,16,10,128]{3,1,2,0:T(8,128)S(1)} %copy.166), channel_id=1, source_target_pairs={{0,64},{64,128},{128,192},{1,65},{65,129},{129,193},{2,66},{66,130... | collective-permute-start | bytes 737288 | tf_op jit(solution)/shard_map/ppermute | solution.py:35
  117.8 11.7 %collective-permute-start.14 = (f32[3,16,10,128]{3,1,2,0:T(8,128)S(1)}, f32[3,16,10,128]{3,1,2,0:T(8,128)S(1)}, u32[]{:S(2)}, u32[]{:S(2)}) collective-permute-start(f32[3,16,10,128]{3,1,2,0:T(8,128)S(1)} %copy.167), channel_id=1, source_target_pairs={{64,0},{128,64},{192,128},{65,1},{129,65},{193,129},{66,2},{130,66... | collective-permute-start | bytes 737288 | tf_op jit(solution)/shard_map/ppermute | solution.py:36
  119.2 10.5 %collective-permute-start.12 = (f32[8,3,10,128]{3,0,2,1:T(8,128)S(1)}, f32[8,3,10,128]{3,0,2,1:T(8,128)S(1)}, u32[]{:S(2)}, u32[]{:S(2)}) collective-permute-start(f32[8,3,10,128]{3,0,2,1:T(8,128)S(1)} %get-tuple-element.91), channel_id=1, source_target_pairs={{0,8},{8,16},{16,24},{24,32},{32,40},{40,48},{48,56},{1,9},{9,17},... | collective-permute-start | bytes 368648 | tf_op jit(solution)/shard_map/ppermute | solution.py:35
  124.2 6.2 %collective-permute-start.15 = (f32[8,3,10,128]{3,0,2,1:T(8,128)S(1)}, f32[8,3,10,128]{3,0,2,1:T(8,128)S(1)}, u32[]{:S(2)}, u32[]{:S(2)}) collective-permute-start(f32[8,3,10,128]{3,0,2,1:T(8,128)S(1)} %get-tuple-element.92), channel_id=1, source_target_pairs={{8,0},{16,8},{24,16},{32,24},{40,32},{48,40},{56,48},{9,1},{17,9},... | collective-permute-start | bytes 368648 | tf_op jit(solution)/shard_map/ppermute | solution.py:36
  126.2 7.1 %collective-permute-start.16 = (f32[8,16,3,128]{3,0,2,1:T(8,128)S(1)}, f32[8,16,3,128]{3,0,2,1:T(8,128)S(1)}, u32[]{:S(2)}, u32[]{:S(2)}) collective-permute-start(f32[8,16,3,128]{3,0,2,1:T(8,128)S(1)} %get-tuple-element.93), channel_id=1, source_target_pairs={{0,1},{1,2},{2,3},{3,4},{4,5},{5,6},{6,7},{7,0},{8,9},{9,10},{10,1... | collective-permute-start | bytes 589832 | tf_op jit(solution)/shard_map/ppermute | solution.py:54
  128.4 4.8 %collective-permute-start.17 = (f32[8,16,3,128]{3,0,2,1:T(8,128)S(1)}, f32[8,16,3,128]{3,0,2,1:T(8,128)S(1)}, u32[]{:S(2)}, u32[]{:S(2)}) collective-permute-start(f32[8,16,3,128]{3,0,2,1:T(8,128)S(1)} %get-tuple-element.94), channel_id=1, source_target_pairs={{1,0},{2,1},{3,2},{4,3},{5,4},{6,5},{7,6},{0,7},{9,8},{10,9},{11,1... | collective-permute-start | bytes 589832 | tf_op jit(solution)/shard_map/ppermute | solution.py:56
  (7 other events, 9.7 us)
where the time goes:
time: 155 us; the launch traced here: 153 us
  other arithmetic  71.9 us (46%)
  starting transfers between devices  55.3 us (36%)
  local copies, waits for them, and re-layouts  19.3 us (12%)
  waiting for transfers between devices  4.98 us (3%)
    ppermute x6, starting transfers between devices, extended_2(): lax.ppermute(last, axis, up)  25 us
    add x1, other arithmetic, body(): level_set + time_step * slope_field(level_set, around_heads(level_set), 0)  18.9 us
    sub x1, other arithmetic, body(): return advanced - level_set  18.5 us
    add x1, other arithmetic, body(): 0.75 * level_set  18.4 us
    ppermute x6, starting transfers between devices, extended_2(): lax.ppermute(initial, axis, [(b, a) for a, b in up])  10.2 us
    all_to_all x1, starting transfers between devices, from_everyone(): return lax.all_to_all(copies, axis, split_axis=0, concat_axis=0, tiled=True)  8.44 us
    ppermute x3, starting transfers between devices, with_halo(): lax.ppermute(head, axis, [((i + 1) % count, i) for i in range(count)])  7.67 us
    unnamed x26, local copies, waits for them, and re-layouts  5.3 us
  transfers between devices with their start and end apart: 19, of which 4 were waited for; matrix products, arithmetic and copies ran while one was open for 15% of the time, Pallas kernels for 0%

commit v1 on v0

v1 whole, which is shorter than its diff:
```python
import functools
import math

import jax
import jax.numpy as jnp
import numpy as np
from jax import lax
from jax.experimental import pallas as pl
from jax.experimental.pallas import tpu as pltpu
from jax.sharding import PartitionSpec as P

CELL_SIZE = 0.05
SPEED_LOW = 0.1
SPEED_SPAN = 0.4
TURN_MAX = 1.0
ACCEL_MAX = 0.05
CFL_NUMBER = 0.5
WENO_EPS = 1e-06
SCALE = 64.0
MESH = pl.DeviceIdType.MESH


def eps_of(spacing):
    return 0.75 * WENO_EPS * (spacing * SCALE) ** 2


def one_side(b1, b2, b3, t1, t2):
    c1 = 3.0 * b1
    c3 = b3 + b3
    return b2 * (c3 * t1 + c1 * t2) / (b2 * (b3 + c1) + c1 * c3)


def both_sides(p, c, m, ta, tb):
    x = m * ta
    y = p * tb
    twice = 2.0 * (x + y)
    p2 = p + p
    m2 = m + m
    total = p + m
    far = 3.0 * (p2 * m)
    left = c * (twice + y) / (c * (total + p2) + far)
    right = c * (twice + x) / (c * (total + m2) + far)
    return left, right


def along(u, eps):
    n = len(u)
    q = [u[k + 1] - u[k] for k in range(n - 1)]
    d = [q[k + 1] - q[k] for k in range(n - 2)]
    s = [None] + [d[k] - d[k - 1] for k in range(1, n - 2)]
    t = [None] + [s[k + 1] - s[k] for k in range(1, n - 3)]
    z = [1.5 * (e * e) for e in d]
    p, c, m = [None], [None], [None]
    for k in range(1, n - 2):
        v = s[k] * s[k] + eps
        x = 0.75 * (d[k - 1] * d[k])
        w = v - x
        c.append(v + x)
        p.append(w + z[k])
        m.append(w + z[k - 1])
    return d, s, t, p, c, m


def kernel(
    sizes,
    u_hbm,
    wind,
    out_hbm,
    u0,
    u1,
    u2,
    acc,
    fx2,
    fx6,
    fy2,
    fy6,
    xlo,
    xhi,
    hlo,
    hhi,
    ylo,
    yhi,
    ysend,
    cos_t,
    sin_t,
    wx,
    wy,
    step_buf,
    top_x,
    top_y,
    top_send,
    out_v,
    in_sem,
    out_sem,
    x_send,
    x_recv,
    h_send,
    h_recv,
    y_send,
    y_recv,
    top_send_sem,
    top_recv_sem,
):
    gx_n, gy_n, ha_n, nx, nh, ny, nv = sizes
    n_head = nh * ha_n
    d_theta = 2.0 * math.pi / n_head
    d_speed = SPEED_SPAN / nv
    gx, gy, ha = lax.axis_index("gx"), lax.axis_index("gy"), lax.axis_index("ha")
    below_x, above_x = gx > 0, gx < gx_n - 1
    below_y, above_y = gy > 0, gy < gy_n - 1
    h_up, h_down = lax.rem(ha + 1, ha_n), lax.rem(ha + ha_n - 1, ha_n)
    us = (u0, u1, u2)
    halves = ny // 8

    load_in = pltpu.make_async_copy(u_hbm, acc, in_sem.at[0])
    load_in.start()

    barrier = pltpu.get_barrier_semaphore()
    for k in range(1, gx_n):
        pl.semaphore_signal(barrier, inc=1, device_id={"gx": lax.rem(gx + k, gx_n)}, device_id_type=MESH)
    for k in range(1, gy_n):
        pl.semaphore_signal(barrier, inc=1, device_id={"gy": lax.rem(gy + k, gy_n)}, device_id_type=MESH)
    pl.semaphore_signal(barrier, inc=1, device_id={"ha": h_up}, device_id_type=MESH)
    pl.semaphore_signal(barrier, inc=1, device_id={"ha": h_down}, device_id_type=MESH)

    def rows(h):
        return pl.ds(8 + 8 * h, 8)

    def inner(h):
        return pl.ds(8 * h, 8)

    def x_copies(s, h):
        u = us[s]
        down = pltpu.make_async_remote_copy(
            src_ref=u.at[pl.ds(0, 3), :, rows(h), :], dst_ref=xhi.at[s, h],
            send_sem=x_send.at[s, h, 0], recv_sem=x_recv.at[s, h, 0],
            device_id={"gx": gx - 1}, device_id_type=MESH)
        up = pltpu.make_async_remote_copy(
            src_ref=u.at[pl.ds(nx - 3, 3), :, rows(h), :], dst_ref=xlo.at[s, h],
            send_sem=x_send.at[s, h, 1], recv_sem=x_recv.at[s, h, 1],
            device_id={"gx": gx + 1}, device_id_type=MESH)
        return down, up

    def h_copies(s, h):
        u = us[s]
        down = pltpu.make_async_remote_copy(
            src_ref=u.at[:, pl.ds(0, 3), rows(h), :], dst_ref=hhi.at[s, h],
            send_sem=h_send.at[s, h, 0], recv_sem=h_recv.at[s, h, 0],
            device_id={"ha": h_down}, device_id_type=MESH)
        up = pltpu.make_async_remote_copy(
            src_ref=u.at[:, pl.ds(nh - 3, 3), rows(h), :], dst_ref=hlo.at[s, h],
            send_sem=h_send.at[s, h, 1], recv_sem=h_recv.at[s, h, 1],
            device_id={"ha": h_up}, device_id_type=MESH)
        return down, up

    def y_copies(s):
        down = pltpu.make_async_remote_copy(
            src_ref=ysend.at[s, 0], dst_ref=yhi.at[s],
            send_sem=y_send.at[s, 0], recv_sem=y_recv.at[s, 0],
            device_id={"gy": gy - 1}, device_id_type=MESH)
        up = pltpu.make_async_remote_copy(
            src_ref=ysend.at[s, 1], dst_ref=ylo.at[s],
            send_sem=y_send.at[s, 1], recv_sem=y_recv.at[s, 1],
            device_id={"gy": gy + 1}, device_id_type=MESH)
        return down, up

    def start_half(s, h):
        down, up = x_copies(s, h)
        pl.when(below_x)(down.start)
        pl.when(above_x)(up.start)
        down, up = h_copies(s, h)
        down.start()
        up.start()
        copies = y_copies(s)
        if h == 0:
            pl.when(below_y)(copies[0].start)
        if h == halves - 1:
            pl.when(above_y)(copies[1].start)

    angles = lax.broadcasted_iota(jnp.int32, (n_head, nv), 0).astype(jnp.float32) * d_theta
    cos_t[...] = jnp.cos(angles)
    sin_t[...] = jnp.sin(angles)
    diagonal = lax.broadcasted_iota(jnp.int32, (ny, ny), 0) == lax.broadcasted_iota(jnp.int32, (ny, ny), 1)
    for i in range(nx):
        for part, out in ((0, wx), (1, wy)):
            row = jnp.broadcast_to(wind[part, pl.ds(i, 1), :], (ny, ny))
            column = jnp.sum(jnp.where(diagonal, row, 0.0), axis=1, keepdims=True)
            out[i] = jnp.broadcast_to(column, (ny, nv))

    low = np.float32(SPEED_LOW) + np.float32(SPEED_SPAN) * np.float32(0.5) / np.float32(nv)
    high = np.float32(SPEED_LOW) + np.float32(SPEED_SPAN) * np.float32(nv - 0.5) / np.float32(nv)
    wind_x, wind_y = wind[0], wind[1]

    def rate_of(k, top):
        c = jnp.broadcast_to(cos_t[pl.ds(k, 1), 0:ny], (nx, ny))
        n = jnp.broadcast_to(sin_t[pl.ds(k, 1), 0:ny], (nx, ny))
        for speed in (float(low), float(high)):
            top = jnp.maximum(top, jnp.abs(speed * c + wind_x) + jnp.abs(speed * n + wind_y))
        return top

    top = lax.fori_loop(0, n_head, rate_of, jnp.zeros((nx, ny), jnp.float32), unroll=4)
    top_send[0] = jnp.full((8, nv), jnp.max(top), jnp.float32)

    speeds = SPEED_LOW + SPEED_SPAN * (
        lax.broadcasted_iota(jnp.int32, (1, nv), 1).astype(jnp.float32) + 0.5) / nv

    def flow_of(j, carry):
        c = speeds * cos_t[pl.ds(ha * nh + j, 1), :]
        n = speeds * sin_t[pl.ds(ha * nh + j, 1), :]
        for i in range(nx):
            f = c + wx[i]
            fx2[i, j] = f * (0.5 / CELL_SIZE)
            fx6[i, j] = jnp.abs(f) * (1.0 / (6.0 * CELL_SIZE))
            f = n + wy[i]
            fy2[i, j] = f * (0.5 / CELL_SIZE)
            fy6[i, j] = jnp.abs(f) * (1.0 / (6.0 * CELL_SIZE))
        return carry

    lax.fori_loop(0, nh, flow_of, 0)

    load_in.wait()

    def pack_y(s, i):
        u = us[s]
        for j in range(nh):
            ysend[s, 0, i, pl.ds(3 * j, 3), :] = u[i, j, pl.ds(8, 3), :]
            ysend[s, 1, i, pl.ds(3 * j, 3), :] = u[i, j, pl.ds(8 + ny - 3, 3), :]

    def scale_in(i, carry):
        for j in range(nh):
            u0[i, j, pl.ds(8, ny), :] = acc[i, j] * SCALE
        return carry

    lax.fori_loop(0, nx, scale_in, 0)

    def pack_all(s):
        def body(i, carry):
            pack_y(s, i)
            return carry
        lax.fori_loop(0, nx, body, 0)

    pack_all(0)

    pl.semaphore_wait(barrier, gx_n - 1 + gy_n - 1 + 2)
    for h in range(halves):
        start_half(0, h)

    def top_copy(axis, me, size, k, phase):
        buf = (top_x, top_y)[phase]
        return pltpu.make_async_remote_copy(
            src_ref=top_send.at[phase], dst_ref=buf.at[k - 1],
            send_sem=top_send_sem.at[phase, k - 1], recv_sem=top_recv_sem.at[phase, k - 1],
            device_id={axis: lax.rem(me + k, size)}, device_id_type=MESH)

    top_copies = [
        [top_copy("gx", gx, gx_n, k, 0) for k in range(1, gx_n)],
        [top_copy("gy", gy, gy_n, k, 1) for k in range(1, gy_n)],
    ]
    for copy in top_copies[0]:
        copy.start()

    lane = lax.broadcasted_iota(jnp.int32, (8, nv), 1)
    first, last = lane == 0, lane == nv - 1

    def v_term(u):
        eps = eps_of(d_speed)
        e2 = eps * eps
        a = pltpu.roll(u, nv - 1, 1) - u
        b = u - pltpu.roll(u, 1, 1)
        q1 = jnp.where(last, b, a)
        q0 = jnp.where(first, a, b)
        d3 = 3.0 * (q0 + q1)
        d = q1 - q0
        dm = pltpu.roll(d, 1, 1)
        s = d - dm
        ta = s - pltpu.roll(s, 1, 1)
        tb = pltpu.roll(ta, nv - 1, 1)
        v = s * s + eps
        x = 0.75 * (d * dm)
        w = v - x
        c = v + x
        p = w + 1.5 * (d * d)
        m = w + 1.5 * (dm * dm)
        p = pltpu.roll(p * p, 1, 1)
        m = pltpu.roll(m * m, nv - 1, 1)
        c = c * c
        left = one_side(jnp.where(first, e2, p), c, m, jnp.where(first, 0.0, ta), tb)
        right = one_side(jnp.where(first, e2, m), c, p, jnp.where(first, 0.0, tb), ta)
        right = pltpu.roll(right - s, nv - 1, 1)
        return (ACCEL_MAX / (6.0 * d_speed)) * jnp.maximum(d3 + right, left + s - d3)

    def v_pass(s):
        u = us[s]

        def body(i, carry):
            for j in range(nh):
                for h in range(halves):
                    acc[i, j, inner(h), :] = v_term(u[i, j, rows(h), :])
            return carry

        lax.fori_loop(0, nx, body, 0)

    def h_pass(s, h):
        u = us[s]
        factor = TURN_MAX / (6.0 * d_theta)

        def body(i, carry):
            cells = [hlo[s, h, i, k] for k in range(3)]
            cells += [u[i, k, rows(h), :] for k in range(nh)]
            cells += [hhi[s, h, i, k] for k in range(3)]
            d, sd, t, p, c, m = along(cells, eps_of(d_theta))
            square = lambda r: [None] + [e * e for e in r[1:]]
            p, c, m = square(p), square(c), square(m)
            sides = {}
            for k in range(2, nh + 3):
                sides[k] = both_sides(p[k - 1], c[k], m[k + 1], t[k - 1], t[k])
            for j in range(nh):
                k = j + 2
                d3 = 3.0 * (cells[j + 4] - cells[j + 2])
                value = jnp.maximum(d3 + (sides[k + 1][1] - sd[k + 1]), (sides[k][0] + sd[k]) - d3)
                acc[i, j, inner(h), :] += factor * value
            return carry

        lax.fori_loop(0, nx, body, 0)

    def x_pass(s, h):
        u = us[s]

        def body(j, carry):
            cells = [xlo[s, h, k, j] for k in range(3)]
            cells += [u[k, j, rows(h), :] for k in range(nx)]
            cells += [xhi[s, h, k, j] for k in range(3)]
            d, sd, t, p, c, m = along(cells, eps_of(CELL_SIZE))
            for i in range(nx):
                k = i + 2
                f2 = fx2[i, j, inner(h), :]
                ahead = f2 > 0.0
                b1 = jnp.where(ahead, m[k + 2], p[k - 1])
                b2 = jnp.where(ahead, c[k + 1], c[k])
                b3 = jnp.where(ahead, p[k], m[k + 1])
                t1 = jnp.where(ahead, t[k + 1], t[k - 1])
                dd = d[k] - jnp.where(ahead, d[k + 1], d[k - 1])
                fix = one_side(b1 * b1, b2 * b2, b3 * b3, t1, t[k])
                acc[i, j, inner(h), :] += f2 * (cells[i + 4] - cells[i + 2]) + fx6[i, j, inner(h), :] * (dd + fix)
            return carry

        lax.fori_loop(0, nh, body, 0)

    def y_term(u, i, j, h):
        eps = eps_of(CELL_SIZE)
        f2 = fy2[i, j, inner(h), :]
        ahead = f2 > 0.0
        cells = [u[i, j, pl.ds(8 + 8 * h + r, 8), :] for r in range(-3, 4)]
        q = [cells[k + 1] - cells[k] for k in range(6)]
        d = [q[k + 1] - q[k] for k in range(5)]
        e1 = jnp.where(ahead, d[4], d[0])
        e2 = jnp.where(ahead, d[3], d[1])
        e3 = d[2]
        e4 = jnp.where(ahead, d[1], d[3])
        s1, s2, s3 = e2 - e1, e3 - e2, e4 - e3
        e2k, e3k = 0.75 * e2, 0.75 * e3
        b1 = (s1 * s1 + eps) + e2k * (e2 + s1)
        b2 = (s2 * s2 + eps) + e2k * e3
        b3 = (s3 * s3 + eps) + e3k * (e3 - s3)
        fix = one_side(b1 * b1, b2 * b2, b3 * b3, s2 - s1, s3 - s2)
        return f2 * (cells[4] - cells[2]) + fy6[i, j, inner(h), :] * (s2 + fix)

    def y_pass(s, h):
        u = us[s]
        dt = step_buf[...]

        def body(i, carry):
            for j in range(nh):
                total = acc[i, j, inner(h), :] + y_term(u, i, j, h)
                change = dt * jnp.minimum(total, 0.0)
                if s == 0:
                    u1[i, j, rows(h), :] = u0[i, j, rows(h), :] + change
                elif s == 1:
                    u2[i, j, rows(h), :] = 0.75 * u0[i, j, rows(h), :] + 0.25 * (u1[i, j, rows(h), :] + change)
                else:
                    out_v[i, j, inner(h), :] = (2.0 / 3.0 / SCALE) * ((u2[i, j, rows(h), :] - u0[i, j, rows(h), :]) + change)
            return carry

        lax.fori_loop(0, nx, body, 0)

    def receive_x(s, h):
        u = us[s]
        down, up = x_copies(s, h)
        pl.when(above_x)(down.wait_recv)
        pl.when(below_x)(up.wait_recv)

        @pl.when(jnp.logical_not(below_x))
        def _():
            def body(j, carry):
                edge = u[0, j, rows(h), :]
                slope = edge - u[1, j, rows(h), :]
                for r in (1, 2, 3):
                    xlo[s, h, 3 - r, j] = edge + float(r) * slope
                return carry
            lax.fori_loop(0, nh, body, 0)

        @pl.when(jnp.logical_not(above_x))
        def _():
            def body(j, carry):
                edge = u[nx - 1, j, rows(h), :]
                slope = edge - u[nx - 2, j, rows(h), :]
                for r in (1, 2, 3):
                    xhi[s, h, r - 1, j] = edge + float(r) * slope
                return carry
            lax.fori_loop(0, nh, body, 0)

    def receive_h(s, h):
        for copy in h_copies(s, h):
            copy.wait_recv()

    def receive_y(s, which):
        u = us[s]
        copy = y_copies(s)[which]
        there = (above_y, below_y)[which]

        @pl.when(there)
        def _():
            copy.wait_recv()

            def body(i, carry):
                for j in range(nh):
                    if which == 0:
                        u[i, j, pl.ds(8 + ny, 3), :] = yhi[s, i, pl.ds(3 * j, 3), :]
                    else:
                        u[i, j, pl.ds(5, 3), :] = ylo[s, i, pl.ds(3 * j, 3), :]
                return carry
            lax.fori_loop(0, nx, body, 0)

        @pl.when(jnp.logical_not(there))
        def _():
            def body(i, carry):
                for j in range(nh):
                    if which == 0:
                        edge = u[i, j, pl.ds(8 + ny - 1, 1), :]
                        slope = edge - u[i, j, pl.ds(8 + ny - 2, 1), :]
                        for r in (1, 2, 3):
                            u[i, j, pl.ds(8 + ny - 1 + r, 1), :] = edge + float(r) * slope
                    else:
                        edge = u[i, j, pl.ds(8, 1), :]
                        slope = edge - u[i, j, pl.ds(9, 1), :]
                        for r in (1, 2, 3):
                            u[i, j, pl.ds(8 - r, 1), :] = edge + float(r) * slope
                return carry
            lax.fori_loop(0, nx, body, 0)

    out_copies = []
    for s in range(3):
        v_pass(s)
        if s == 0:
            for copy in top_copies[0]:
                copy.wait_recv()
            best = top_send[0]
            for k in range(1, gx_n):
                best = jnp.maximum(best, top_x[k - 1])
            top_send[1] = best
            for copy in top_copies[1]:
                copy.start()
        for h in range(halves):
            receive_h(s, h)
            h_pass(s, h)
            receive_x(s, h)
            x_pass(s, h)
            if h == 0:
                receive_y(s, 1)
            if h == halves - 1:
                receive_y(s, 0)
            if s == 0 and h == 0:
                for copy in top_copies[1]:
                    copy.wait_recv()
                best = top_send[1]
                for k in range(1, gy_n):
                    best = jnp.maximum(best, top_y[k - 1])
                rate = best / CELL_SIZE + (TURN_MAX / d_theta + ACCEL_MAX / d_speed)
                step_buf[...] = CFL_NUMBER / rate
            y_pass(s, h)
            if s < 2:
                def pack(i, carry, s=s, h=h):
                    for j in range(nh):
                        if h == 0:
                            ysend[s + 1, 0, i, pl.ds(3 * j, 3), :] = us[s + 1][i, j, pl.ds(8, 3), :]
                        if h == halves - 1:
                            ysend[s + 1, 1, i, pl.ds(3 * j, 3), :] = us[s + 1][i, j, pl.ds(8 + ny - 3, 3), :]
                    return carry
                lax.fori_loop(0, nx, pack, 0)
                start_half(s + 1, h)
            else:
                copy = pltpu.make_async_copy(
                    out_v.at[:, :, inner(h), :], out_hbm.at[:, :, inner(h), :], out_sem.at[h])
                copy.start()
                out_copies.append(copy)

    for copy in top_copies[0] + top_copies[1]:
        copy.wait_send()
    for s in range(3):
        for h in range(halves):
            down, up = x_copies(s, h)
            pl.when(below_x)(down.wait_send)
            pl.when(above_x)(up.wait_send)
            for copy in h_copies(s, h):
                copy.wait_send()
        down, up = y_copies(s)
        pl.when(below_y)(down.wait_send)
        pl.when(above_y)(up.wait_send)
    for copy in out_copies:
        copy.wait()


def solution(mesh):
    gx_n, gy_n, ha_n = mesh.shape["gx"], mesh.shape["gy"], mesh.shape["ha"]

    def body(level_set, wind_field):
        nx, ny, nh, nv = level_set.shape
        halves = ny // 8
        f32 = jnp.float32
        field = pltpu.VMEM((nx, nh, ny + 16, nv), f32)
        plain = pltpu.VMEM((nx, nh, ny, nv), f32)
        y_rows = -(-3 * nh // 8) * 8
        dma = pltpu.SemaphoreType.DMA
        block = jnp.transpose(level_set, (0, 2, 1, 3))
        out = pl.pallas_call(
            functools.partial(kernel, (gx_n, gy_n, ha_n, nx, nh, ny, nv)),
            out_shape=jax.ShapeDtypeStruct(block.shape, f32),
            in_specs=[
                pl.BlockSpec(memory_space=pl.ANY),
                pl.BlockSpec(memory_space=pltpu.VMEM),
            ],
            out_specs=pl.BlockSpec(memory_space=pl.ANY),
            scratch_shapes=[
                field, field, field,
                plain, plain, plain, plain, plain,
                pltpu.VMEM((3, halves, 3, nh, 8, nv), f32),
                pltpu.VMEM((3, halves, 3, nh, 8, nv), f32),
                pltpu.VMEM((3, halves, nx, 3, 8, nv), f32),
                pltpu.VMEM((3, halves, nx, 3, 8, nv), f32),
                pltpu.VMEM((3, nx, y_rows, nv), f32),
                pltpu.VMEM((3, nx, y_rows, nv), f32),
                pltpu.VMEM((3, 2, nx, y_rows, nv), f32),
                pltpu.VMEM((nh * ha_n, nv), f32),
                pltpu.VMEM((nh * ha_n, nv), f32),
                pltpu.VMEM((nx, ny, nv), f32),
                pltpu.VMEM((nx, ny, nv), f32),
                pltpu.VMEM((8, nv), f32),
                pltpu.VMEM((gx_n - 1, 8, nv), f32),
                pltpu.VMEM((gy_n - 1, 8, nv), f32),
                pltpu.VMEM((2, 8, nv), f32),
                plain,
                dma((1,)), dma((halves,)),
                dma((3, halves, 2)), dma((3, halves, 2)),
                dma((3, halves, 2)), dma((3, halves, 2)),
                dma((3, 2)), dma((3, 2)),
                dma((2, max(gx_n, gy_n))), dma((2, max(gx_n, gy_n))),
            ],
            compiler_params=pltpu.CompilerParams(collective_id=0, has_side_effects=True),
        )(block, wind_field)
        return jnp.transpose(out, (0, 2, 1, 3))

    return jax.shard_map(
        body,
        mesh=mesh,
        in_specs=(P("gx", "gy", "ha", None), P(None, "gx", "gy")),
        out_specs=P("gx", "gy", "ha", None),
        check_vma=False,
    )
```

time: 155 us -> 44.3 us (0.29); the launches traced: 153 us -> 44.1 us
  other arithmetic: 71.9 us -> 0 us
  starting transfers between devices: 55.3 us -> 0 us
  Pallas kernels: 0 us -> 42.1 us
  local copies, waits for them, and re-layouts: 19.3 us -> 1.97 us
  waiting for transfers between devices: 4.98 us -> 0 us
    ppermute x18 -> x0, starting transfers between devices: 46.8 us -> none  [the longest x6 25 us: extended_2(): lax.ppermute(last, axis, up)]
    add x15 -> x0, other arithmetic: 42.6 us -> none  [the longest x1 18.9 us: body(): level_set + time_step * slope_field(level_set, around_heads(level_set), 0)]
    pallas_call x0 -> x1, Pallas kernels: none -> 42.1 us  [body(): pl.pallas_call(functools.partial(kernel, (gx_n, gy_n, ha_n, nx, nh, ny, n...]
    sub x1 -> x0, other arithmetic: 18.5 us -> none  [body(): return advanced - level_set]
    slice x29 -> x0, local copies, waits for them, and re-layouts: 9.2 us -> none  [the longest x9 5.21 us: speed_shifts(): lax.slice_in_dim(values, max(displace, 0), length + min(displace, 0), axi...]
    all_to_all x1 -> x0, starting transfers between devices: 8.44 us -> none  [from_everyone(): return lax.all_to_all(copies, axis, split_axis=0, concat_axis=0, tiled=True)]
    ppermute x18 -> x0, waiting for transfers between devices: 4.98 us -> none  [the longest x3 2.93 us: with_halo(): lax.ppermute(head, axis, [((i + 1) % count, i) for i in range(count)])]
    concatenate x6 -> x0, other arithmetic: 3.95 us -> none  [the longest x3 2.07 us: fix_edges(): return jnp.concatenate([below_rows, interior, above_rows], axis=along)]
  transfers between devices with their start and end apart: 19 -> 0, of which waited for: 4 -> 0; matrix products, arithmetic and copies ran while one was open for 15% -> 0% of each run, Pallas kernels for 0% -> 0%
where the time goes in v1:
time: 44.3 us; the launch traced here: 44.1 us
  Pallas kernels  42.1 us (95%)
  local copies, waits for them, and re-layouts  1.97 us (4%)
    pallas_call x1, Pallas kernels, body(): pl.pallas_call(functools.partial(kernel, (gx_n, gy_n, ha_n, nx, nh, ny, n...  42.1 us
    unnamed x1, local copies, waits for them, and re-layouts  1.97 us

profile of v1, /device:TPU:1, one launch (start us, length us, event | category | flops | bytes accessed | tf_op | source)
XLA Modules:
  0.0 44.1 jit_solution(13958492750833952715)
XLA Ops:
  0.0 42.1 %shard_map.28 = f32[8,10,16,128]{3,2,1,0:T(8,128)} custom-call(f32[8,10,16,128]{3,2,1,0:T(8,128)} %bitcast.3, f32[2,8,16]{2,1,0:T(8,128)} %wind.1), custom_call_target="tpu_custom_call" | custom-call | tf_op jit(solution)/shard_map/pallas_call | solution.py:525
  42.1 2.0 %copy.4 = f32[8,16,10,128]{3,1,2,0:T(8,128)} copy(f32[8,16,10,128]{3,1,2,0:T(8,128)} %bitcast.2) | data formatting | bytes 1310720

commit v2 on v1

--- a/solution.py
+++ b/solution.py
@@ -17,6 +17,8 @@
 CFL_NUMBER = 0.5
 WENO_EPS = 1e-06
 SCALE = 64.0
+VMEM_LIMIT = 40 * 2**20
+V_APART = 2
 MESH = pl.DeviceIdType.MESH
 
 
@@ -64,11 +66,10 @@
 def kernel(
     sizes,
     u_hbm,
+    wind_hbm,
+    out_ref,
     wind,
-    out_hbm,
-    u0,
-    u1,
-    u2,
+    us,
     acc,
     fx2,
     fx6,
@@ -86,12 +87,18 @@
     wx,
     wy,
     step_buf,
+    vd,
+    vq,
+    vs,
+    vc,
+    vp,
+    vm,
+    vl,
+    vr,
     top_x,
     top_y,
     top_send,
-    out_v,
     in_sem,
-    out_sem,
     x_send,
     x_recv,
     h_send,
@@ -109,10 +116,11 @@
     below_x, above_x = gx > 0, gx < gx_n - 1
     below_y, above_y = gy > 0, gy < gy_n - 1
     h_up, h_down = lax.rem(ha + 1, ha_n), lax.rem(ha + ha_n - 1, ha_n)
-    us = (u0, u1, u2)
     halves = ny // 8
 
     load_in = pltpu.make_async_copy(u_hbm, acc, in_sem.at[0])
+    load_wind = pltpu.make_async_copy(wind_hbm, wind, in_sem.at[1])
+    load_wind.start()
     load_in.start()
 
     barrier = pltpu.get_barrier_semaphore()
@@ -130,7 +138,7 @@
         return pl.ds(8 * h, 8)
 
     def x_copies(s, h):
-        u = us[s]
+        u = us.at[s]
         down = pltpu.make_async_remote_copy(
             src_ref=u.at[pl.ds(0, 3), :, rows(h), :], dst_ref=xhi.at[s, h],
             send_sem=x_send.at[s, h, 0], recv_sem=x_recv.at[s, h, 0],
@@ -142,7 +150,7 @@
         return down, up
 
     def h_copies(s, h):
-        u = us[s]
+        u = us.at[s]
         down = pltpu.make_async_remote_copy(
             src_ref=u.at[:, pl.ds(0, 3), rows(h), :], dst_ref=hhi.at[s, h],
             send_sem=h_send.at[s, h, 0], recv_sem=h_recv.at[s, h, 0],
@@ -180,6 +188,7 @@
     angles = lax.broadcasted_iota(jnp.int32, (n_head, nv), 0).astype(jnp.float32) * d_theta
     cos_t[...] = jnp.cos(angles)
     sin_t[...] = jnp.sin(angles)
+    load_wind.wait()
     diagonal = lax.broadcasted_iota(jnp.int32, (ny, ny), 0) == lax.broadcasted_iota(jnp.int32, (ny, ny), 1)
     for i in range(nx):
         for part, out in ((0, wx), (1, wy)):
@@ -216,19 +225,17 @@
             fy6[i, j] = jnp.abs(f) * (1.0 / (6.0 * CELL_SIZE))
         return carry
 
-    lax.fori_loop(0, nh, flow_of, 0)
-
     load_in.wait()
 
     def pack_y(s, i):
-        u = us[s]
+        u = us.at[s]
         for j in range(nh):
             ysend[s, 0, i, pl.ds(3 * j, 3), :] = u[i, j, pl.ds(8, 3), :]
             ysend[s, 1, i, pl.ds(3 * j, 3), :] = u[i, j, pl.ds(8 + ny - 3, 3), :]
 
     def scale_in(i, carry):
         for j in range(nh):
-            u0[i, j, pl.ds(8, ny), :] = acc[i, j] * SCALE
+            us[0, i, j, pl.ds(8, ny), :] = acc[i, j] * SCALE
         return carry
 
     lax.fori_loop(0, nx, scale_in, 0)
@@ -242,8 +249,6 @@
     pack_all(0)
 
     pl.semaphore_wait(barrier, gx_n - 1 + gy_n - 1 + 2)
-    for h in range(halves):
-        start_half(0, h)
 
     def top_copy(axis, me, size, k, phase):
         buf = (top_x, top_y)[phase]
@@ -258,50 +263,70 @@
     ]
     for copy in top_copies[0]:
         copy.start()
-
-    lane = lax.broadcasted_iota(jnp.int32, (8, nv), 1)
-    first, last = lane == 0, lane == nv - 1
-
-    def v_term(u):
+    for h in range(halves):
+        start_half(0, h)
+    lax.fori_loop(0, nh, flow_of, 0)
+
+    def v_pass(s):
+        u = us.at[s]
         eps = eps_of(d_speed)
         e2 = eps * eps
-        a = pltpu.roll(u, nv - 1, 1) - u
-        b = u - pltpu.roll(u, 1, 1)
-        q1 = jnp.where(last, b, a)
-        q0 = jnp.where(first, a, b)
-        d3 = 3.0 * (q0 + q1)
-        d = q1 - q0
-        dm = pltpu.roll(d, 1, 1)
-        s = d - dm
-        ta = s - pltpu.roll(s, 1, 1)
-        tb = pltpu.roll(ta, nv - 1, 1)
-        v = s * s + eps
-        x = 0.75 * (d * dm)
-        w = v - x
-        c = v + x
-        p = w + 1.5 * (d * d)
-        m = w + 1.5 * (dm * dm)
-        p = pltpu.roll(p * p, 1, 1)
-        m = pltpu.roll(m * m, nv - 1, 1)
-        c = c * c
-        left = one_side(jnp.where(first, e2, p), c, m, jnp.where(first, 0.0, ta), tb)
-        right = one_side(jnp.where(first, e2, m), c, p, jnp.where(first, 0.0, tb), ta)
-        right = pltpu.roll(right - s, nv - 1, 1)
-        return (ACCEL_MAX / (6.0 * d_speed)) * jnp.maximum(d3 + right, left + s - d3)
-
-    def v_pass(s):
-        u = us[s]
-
-        def body(i, carry):
-            for j in range(nh):
-                for h in range(halves):
-                    acc[i, j, inner(h), :] = v_term(u[i, j, rows(h), :])
-            return carry
-
-        lax.fori_loop(0, nx, body, 0)
+        factor = ACCEL_MAX / (6.0 * d_speed)
+        blocks = [(i, h) for i in range(nx) for h in range(halves)]
+        shape = (nh, 8, nv)
+        lane = lax.broadcasted_iota(jnp.int32, (8, nv), 1)
+        first = jnp.broadcast_to(lane == 0, shape)
+        last = jnp.broadcast_to(lane == nv - 1, shape)
+
+        def level_0(i, h):
+            v = u[i, :, rows(h), :]
+            a = pltpu.roll(v, nv - 1, 2) - v
+            b = v - pltpu.roll(v, 1, 2)
+            q1 = jnp.where(last, b, a)
+            q0 = jnp.where(first, a, b)
+            vq[i, h] = 3.0 * (q0 + q1)
+            vd[i, h] = q1 - q0
+
+        def level_1(i, h):
+            d = vd[i, h]
+            dm = pltpu.roll(d, 1, 2)
+            s = d - dm
+            c = (s * s + eps) + 0.75 * (d * dm)
+            r = 1.5 * s
+            p = c + r * d
+            m = c - r * dm
+            vs[i, h] = s
+            vc[i, h] = c * c
+            vp[i, h] = p * p
+            vm[i, h] = m * m
+
+        def level_2(i, h):
+            s = vs[i, h]
+            ta = s - pltpu.roll(s, 1, 2)
+            tb = pltpu.roll(s, nv - 1, 2) - s
+            p = pltpu.roll(vp[i, h], 1, 2)
+            m = pltpu.roll(vm[i, h], nv - 1, 2)
+            c = vc[i, h]
+            left = one_side(jnp.where(first, e2, p), c, m, jnp.where(first, 0.0, ta), tb)
+            right = one_side(jnp.where(first, e2, m), c, p, jnp.where(first, 0.0, tb), ta)
+            vl[i, h] = left + s
+            vr[i, h] = right - s
+
+        def level_3(i, h):
+            right = pltpu.roll(vr[i, h], nv - 1, 2)
+            d3 = vq[i, h]
+            acc[i, :, inner(h), :] = factor * jnp.maximum(d3 + right, vl[i, h] - d3)
+
+        levels = (level_0, level_1, level_2, level_3)
+        apart = V_APART
+        for step in range(len(blocks) + apart * (len(levels) - 1)):
+            for n in reversed(range(len(levels))):
+                k = step - apart * n
+                if 0 <= k < len(blocks):
+                    levels[n](*blocks[k])
 
     def h_pass(s, h):
-        u = us[s]
+        u = us.at[s]
         factor = TURN_MAX / (6.0 * d_theta)
 
         def body(i, carry):
@@ -324,7 +349,7 @@
         lax.fori_loop(0, nx, body, 0)
 
     def x_pass(s, h):
-        u = us[s]
+        u = us.at[s]
 
         def body(j, carry):
             cells = [xlo[s, h, k, j] for k in range(3)]
@@ -366,25 +391,41 @@
         return f2 * (cells[4] - cells[2]) + fy6[i, j, inner(h), :] * (s2 + fix)
 
     def y_pass(s, h):
-        u = us[s]
+        u = us.at[s]
         dt = step_buf[...]
-
-        def body(i, carry):
-            for j in range(nh):
-                total = acc[i, j, inner(h), :] + y_term(u, i, j, h)
-                change = dt * jnp.minimum(total, 0.0)
-                if s == 0:
-                    u1[i, j, rows(h), :] = u0[i, j, rows(h), :] + change
-                elif s == 1:
-                    u2[i, j, rows(h), :] = 0.75 * u0[i, j, rows(h), :] + 0.25 * (u1[i, j, rows(h), :] + change)
-                else:
-                    out_v[i, j, inner(h), :] = (2.0 / 3.0 / SCALE) * ((u2[i, j, rows(h), :] - u0[i, j, rows(h), :]) + change)
-            return carry
-
-        lax.fori_loop(0, nx, body, 0)
+        keep = jnp.where(s == 1, 0.75, 0.0)
+        take = jnp.where(s == 1, 0.25, 1.0)
+
+        def change(i, j):
+            total = acc[i, j, inner(h), :] + y_term(u, i, j, h)
+            return u[i, j, rows(h), :] + dt * jnp.minimum(total, 0.0)
+
+        @pl.when(s < 2)
+        def _():
+            def body(i, carry):
+                fresh = [keep * us[0, i, j, rows(h), :] + take * change(i, j) for j in range(nh)]
+                for j in range(nh):
+                    us[s + 1, i, j, rows(h), :] = fresh[j]
+                    if h == 0:
+                        ysend[s + 1, 0, i, pl.ds(3 * j, 3), :] = fresh[j][0:3]
+                    if h == halves - 1:
+                        ysend[s + 1, 1, i, pl.ds(3 * j, 3), :] = fresh[j][5:8]
+                return carry
+
+            lax.fori_loop(0, nx, body, 0)
+            start_half(s + 1, h)
+
+        @pl.when(s == 2)
+        def _():
+            def body(i, carry):
+                for j in range(nh):
+                    out_ref[i, j, inner(h), :] = change(i, j) - us[0, i, j, rows(h), :]
+                return carry
+
+            lax.fori_loop(0, nx, body, 0)
 
     def receive_x(s, h):
-        u = us[s]
+        u = us.at[s]
         down, up = x_copies(s, h)
         pl.when(above_x)(down.wait_recv)
         pl.when(below_x)(up.wait_recv)
@@ -414,7 +455,7 @@
             copy.wait_recv()
 
     def receive_y(s, which):
-        u = us[s]
+        u = us.at[s]
         copy = y_copies(s)[which]
         there = (above_y, below_y)[which]
 
@@ -448,10 +489,11 @@
                 return carry
             lax.fori_loop(0, nx, body, 0)
 
-    out_copies = []
-    for s in range(3):
+    def stage(s, carry):
         v_pass(s)
-        if s == 0:
+
+        @pl.when(s == 0)
+        def _():
             for copy in top_copies[0]:
                 copy.wait_recv()
             best = top_send[0]
@@ -460,6 +502,7 @@
             top_send[1] = best
             for copy in top_copies[1]:
                 copy.start()
+
         for h in range(halves):
             receive_h(s, h)
             h_pass(s, h)
@@ -467,32 +510,23 @@
             x_pass(s, h)
             if h == 0:
                 receive_y(s, 1)
+
+                @pl.when(s == 0)
+                def _():
+                    for copy in top_copies[1]:
+                        copy.wait_recv()
+                    best = top_send[1]
+                    for k in range(1, gy_n):
+                        best = jnp.maximum(best, top_y[k - 1])
+                    rate = best / CELL_SIZE + (TURN_MAX / d_theta + ACCEL_MAX / d_speed)
+                    step_buf[...] = CFL_NUMBER / rate
+
             if h == halves - 1:
                 receive_y(s, 0)
-            if s == 0 and h == 0:
-                for copy in top_copies[1]:
-                    copy.wait_recv()
-                best = top_send[1]
-                for k in range(1, gy_n):
-                    best = jnp.maximum(best, top_y[k - 1])
-                rate = best / CELL_SIZE + (TURN_MAX / d_theta + ACCEL_MAX / d_speed)
-                step_buf[...] = CFL_NUMBER / rate
             y_pass(s, h)
-            if s < 2:
-                def pack(i, carry, s=s, h=h):
-                    for j in range(nh):
-                        if h == 0:
-                            ysend[s + 1, 0, i, pl.ds(3 * j, 3), :] = us[s + 1][i, j, pl.ds(8, 3), :]
-                        if h == halves - 1:
-                            ysend[s + 1, 1, i, pl.ds(3 * j, 3), :] = us[s + 1][i, j, pl.ds(8 + ny - 3, 3), :]
-                    return carry
-                lax.fori_loop(0, nx, pack, 0)
-                start_half(s + 1, h)
-            else:
-                copy = pltpu.make_async_copy(
-                    out_v.at[:, :, inner(h), :], out_hbm.at[:, :, inner(h), :], out_sem.at[h])
-                copy.start()
-                out_copies.append(copy)
+        return carry
+
+    lax.fori_loop(0, 3, stage, 0)
 
     for copy in top_copies[0] + top_copies[1]:
         copy.wait_send()
@@ -506,8 +540,6 @@
         down, up = y_copies(s)
         pl.when(below_y)(down.wait_send)
         pl.when(above_y)(up.wait_send)
-    for copy in out_copies:
-        copy.wait()
 
 
 def solution(mesh):
@@ -517,21 +549,23 @@
         nx, ny, nh, nv = level_set.shape
         halves = ny // 8
         f32 = jnp.float32
-        field = pltpu.VMEM((nx, nh, ny + 16, nv), f32)
         plain = pltpu.VMEM((nx, nh, ny, nv), f32)
         y_rows = -(-3 * nh // 8) * 8
+        block_8 = pltpu.VMEM((nx, halves, nh, 8, nv), f32)
         dma = pltpu.SemaphoreType.DMA
-        block = jnp.transpose(level_set, (0, 2, 1, 3))
+        block = pltpu.with_memory_space_constraint(jnp.transpose(level_set, (0, 2, 1, 3)), pltpu.HBM)
+        wind_field = pltpu.with_memory_space_constraint(wind_field, pltpu.HBM)
         out = pl.pallas_call(
             functools.partial(kernel, (gx_n, gy_n, ha_n, nx, nh, ny, nv)),
             out_shape=jax.ShapeDtypeStruct(block.shape, f32),
             in_specs=[
-                pl.BlockSpec(memory_space=pl.ANY),
-                pl.BlockSpec(memory_space=pltpu.VMEM),
+                pl.BlockSpec(memory_space=pltpu.HBM),
+                pl.BlockSpec(memory_space=pltpu.HBM),
             ],
-            out_specs=pl.BlockSpec(memory_space=pl.ANY),
+            out_specs=pl.BlockSpec(memory_space=pltpu.VMEM),
             scratch_shapes=[
-                field, field, field,
+                pltpu.VMEM((2, nx, ny), f32),
+                pltpu.VMEM((3, nx, nh, ny + 16, nv), f32),
                 plain, plain, plain, plain, plain,
                 pltpu.VMEM((3, halves, 3, nh, 8, nv), f32),
                 pltpu.VMEM((3, halves, 3, nh, 8, nv), f32),
@@ -545,19 +579,20 @@
                 pltpu.VMEM((nx, ny, nv), f32),
                 pltpu.VMEM((nx, ny, nv), f32),
                 pltpu.VMEM((8, nv), f32),
+                block_8, block_8, block_8, block_8, block_8, block_8, block_8, block_8,
                 pltpu.VMEM((gx_n - 1, 8, nv), f32),
                 pltpu.VMEM((gy_n - 1, 8, nv), f32),
                 pltpu.VMEM((2, 8, nv), f32),
-                plain,
-                dma((1,)), dma((halves,)),
+                dma((2,)),
                 dma((3, halves, 2)), dma((3, halves, 2)),
                 dma((3, halves, 2)), dma((3, halves, 2)),
                 dma((3, 2)), dma((3, 2)),
                 dma((2, max(gx_n, gy_n))), dma((2, max(gx_n, gy_n))),
             ],
-            compiler_params=pltpu.CompilerParams(collective_id=0, has_side_effects=True),
+            compiler_params=pltpu.CompilerParams(
+                collective_id=0, has_side_effects=True, vmem_limit_bytes=VMEM_LIMIT),
         )(block, wind_field)
-        return jnp.transpose(out, (0, 2, 1, 3))
+        return jnp.transpose(out * (2.0 / 3.0 / SCALE), (0, 2, 1, 3))
 
     return jax.shard_map(
         body,

time: 44.3 us -> 34.8 us (0.79)
  Pallas kernels: 42.1 us -> 33.8 us
  local copies, waits for them, and re-layouts: 1.97 us -> 0 us
  other arithmetic: 0 us -> 0.9 us
    pallas_call x1, Pallas kernels: 42.1 us -> 33.8 us  [body(): pl.pallas_call(functools.partial(kernel, (gx_n, gy_n, ha_n, nx, nh, ny, n...]
    unnamed x1 -> x0, local copies, waits for them, and re-layouts: 1.97 us -> none
    transpose x0 -> x1, other arithmetic: none -> 0.9 us  [body(): return jnp.transpose(out * (2.0 / 3.0 / SCALE), (0, 2, 1, 3))]
where the time goes in v2:
time: 34.8 us; the launch traced here: 34.7 us
  Pallas kernels  33.8 us (97%)
  other arithmetic  0.9 us (3%)
    pallas_call x1, Pallas kernels, body(): pl.pallas_call(functools.partial(kernel, (gx_n, gy_n, ha_n, nx, nh, ny, n...  33.8 us
    transpose x1, other arithmetic, body(): return jnp.transpose(out * (2.0 / 3.0 / SCALE), (0, 2, 1, 3))  0.9 us

profile of v2, /device:TPU:1, one launch (start us, length us, event | category | flops | bytes accessed | tf_op | source)
XLA Modules:
  0.0 34.7 jit_solution(14869391100073089368)
XLA Ops:
  0.0 33.8 %shard_map.28 = f32[8,10,16,128]{3,2,1,0:T(8,128)S(1)} custom-call(f32[8,10,16,128]{3,2,1,0:T(8,128)} %bitcast.3, f32[2,8,16]{2,1,0:T(8,128)} %wind_hbm.1), custom_call_target="tpu_custom_call" | custom-call | tf_op jit(solution)/shard_map/pallas_call | solution.py:558
  33.8 0.9 %multiply_bitcast_fusion = f32[8,16,10,128]{3,1,2,0:T(8,128)} fusion(f32[8,10,16,128]{3,2,1,0:T(8,128)S(1)} %shard_map.28), kind=kLoop, calls=%fused_computation | loop fusion | flops 163840 | bytes 1310720 | tf_op jit(solution)/shard_map/transpose | solution.py:595

commit v3 on v2

--- a/solution.py
+++ b/solution.py
@@ -18,7 +18,8 @@
 WENO_EPS = 1e-06
 SCALE = 64.0
 VMEM_LIMIT = 40 * 2**20
-V_APART = 2
+V_ROWS = 2
+V_APART = 12
 MESH = pl.DeviceIdType.MESH
 
 
@@ -70,6 +71,7 @@
     out_ref,
     wind,
     us,
+    rate_0,
     acc,
     fx2,
     fx6,
@@ -137,78 +139,154 @@
     def inner(h):
         return pl.ds(8 * h, 8)
 
-    def x_copies(s, h):
-        u = us.at[s]
+    def field(s):
+        return (us.at[0], rate_0, us.at[2])[s]
+
+    def parity(s):
+        return s % 2 if isinstance(s, int) else lax.rem(s, 2)
+
+    def base(s):
+        return 0 if s == 1 else 8
+
+    def x_copies(s, h, u=None, start=8):
+        u = us.at[0] if u is None else u
+        place = pl.ds(start + 8 * h, 8)
         down = pltpu.make_async_remote_copy(
-            src_ref=u.at[pl.ds(0, 3), :, rows(h), :], dst_ref=xhi.at[s, h],
-            send_sem=x_send.at[s, h, 0], recv_sem=x_recv.at[s, h, 0],
+            src_ref=u.at[pl.ds(0, 3), :, place, :], dst_ref=xhi.at[s, h],
+            send_sem=x_send.at[h, 0], recv_sem=x_recv.at[parity(s), h, 0],
             device_id={"gx": gx - 1}, device_id_type=MESH)
         up = pltpu.make_async_remote_copy(
-            src_ref=u.at[pl.ds(nx - 3, 3), :, rows(h), :], dst_ref=xlo.at[s, h],
-            send_sem=x_send.at[s, h, 1], recv_sem=x_recv.at[s, h, 1],
+            src_ref=u.at[pl.ds(nx - 3, 3), :, place, :], dst_ref=xlo.at[s, h],
+            send_sem=x_send.at[h, 1], recv_sem=x_recv.at[parity(s), h, 1],
             device_id={"gx": gx + 1}, device_id_type=MESH)
         return down, up
 
-    def h_copies(s, h):
-        u = us.at[s]
+    def h_copies(s, h, u=None, start=8):
+        u = us.at[0] if u is None else u
+        place = pl.ds(start + 8 * h, 8)
         down = pltpu.make_async_remote_copy(
-            src_ref=u.at[:, pl.ds(0, 3), rows(h), :], dst_ref=hhi.at[s, h],
-            send_sem=h_send.at[s, h, 0], recv_sem=h_recv.at[s, h, 0],
+            src_ref=u.at[:, pl.ds(0, 3), place, :], dst_ref=hhi.at[s, h],
+            send_sem=h_send.at[h, 0], recv_sem=h_recv.at[parity(s), h, 0],
             device_id={"ha": h_down}, device_id_type=MESH)
         up = pltpu.make_async_remote_copy(
-            src_ref=u.at[:, pl.ds(nh - 3, 3), rows(h), :], dst_ref=hlo.at[s, h],
-            send_sem=h_send.at[s, h, 1], recv_sem=h_recv.at[s, h, 1],
+            src_ref=u.at[:, pl.ds(nh - 3, 3), place, :], dst_ref=hlo.at[s, h],
+            send_sem=h_send.at[h, 1], recv_sem=h_recv.at[parity(s), h, 1],
             device_id={"ha": h_up}, device_id_type=MESH)
         return down, up
 
     def y_copies(s):
         down = pltpu.make_async_remote_copy(
             src_ref=ysend.at[s, 0], dst_ref=yhi.at[s],
-            send_sem=y_send.at[s, 0], recv_sem=y_recv.at[s, 0],
+            send_sem=y_send.at[0], recv_sem=y_recv.at[parity(s), 0],
             device_id={"gy": gy - 1}, device_id_type=MESH)
         up = pltpu.make_async_remote_copy(
             src_ref=ysend.at[s, 1], dst_ref=ylo.at[s],
-            send_sem=y_send.at[s, 1], recv_sem=y_recv.at[s, 1],
+            send_sem=y_send.at[1], recv_sem=y_recv.at[parity(s), 1],
             device_id={"gy": gy + 1}, device_id_type=MESH)
         return down, up
 
+    def x_sent(s, h):
+        down, up = x_copies(s, h, field(s), base(s))
+        pl.when(below_x)(down.wait_send)
+        pl.when(above_x)(up.wait_send)
+
+    def h_sent(s, h):
+        for copy in h_copies(s, h, field(s), base(s)):
+            copy.wait_send()
+
+    def y_sent(s, which):
+        pl.when((below_y, above_y)[which])(y_copies(s)[which].wait_send)
+
     def start_half(s, h):
-        down, up = x_copies(s, h)
+        if s > 0:
+            x_sent(s - 1, h)
+            h_sent(s - 1, h)
+        down, up = x_copies(s, h, field(s), base(s))
         pl.when(below_x)(down.start)
         pl.when(above_x)(up.start)
-        down, up = h_copies(s, h)
-        down.start()
-        up.start()
-        copies = y_copies(s)
-        if h == 0:
-            pl.when(below_y)(copies[0].start)
-        if h == halves - 1:
-            pl.when(above_y)(copies[1].start)
+        for copy in h_copies(s, h, field(s), base(s)):
+            copy.start()
+
+    def start_y(s, which):
+        if s > 0:
+            y_sent(s - 1, which)
+        pl.when((below_y, above_y)[which])(y_copies(s)[which].start)
 
     angles = lax.broadcasted_iota(jnp.int32, (n_head, nv), 0).astype(jnp.float32) * d_theta
     cos_t[...] = jnp.cos(angles)
     sin_t[...] = jnp.sin(angles)
+
+    load_in.wait()
+
+    def pack_y(s, i):
+        u = us.at[s]
+        for j in range(nh):
+            ysend[s, 0, i, pl.ds(3 * j, 3), :] = u[i, j, pl.ds(8, 3), :]
+            ysend[s, 1, i, pl.ds(3 * j, 3), :] = u[i, j, pl.ds(8 + ny - 3, 3), :]
+
+    def scale_in(i, carry):
+        for j in range(nh):
+            us[0, i, j, pl.ds(8, ny), :] = acc[i, j] * SCALE
+        return carry
+
+    lax.fori_loop(0, nx, scale_in, 0)
+
+    def pack_all(s):
+        def body(i, carry):
+            pack_y(s, i)
+            return carry
+        lax.fori_loop(0, nx, body, 0)
+
+    pack_all(0)
+
+    pl.semaphore_wait(barrier, gx_n - 1 + gy_n - 1 + 2)
+    start_half(0, 0)
+    start_y(0, 0)
+    start_y(0, 1)
+
+    low = np.float32(SPEED_LOW) + np.float32(SPEED_SPAN) * np.float32(0.5) / np.float32(nv)
+    high = np.float32(SPEED_LOW) + np.float32(SPEED_SPAN) * np.float32(nv - 0.5) / np.float32(nv)
     load_wind.wait()
+    wind_x, wind_y = wind[0], wind[1]
+
+    def rate_of(k, top):
+        c = jnp.broadcast_to(cos_t[pl.ds(k, 1), 0:ny], (nx, ny))
+        n = jnp.broadcast_to(sin_t[pl.ds(k, 1), 0:ny], (nx, ny))
+        for speed in (float(low), float(high)):
+            top = jnp.maximum(top, jnp.abs(speed * c + wind_x) + jnp.abs(speed * n + wind_y))
+        return top
+
+    top = lax.fori_loop(0, n_head, rate_of, jnp.zeros((nx, ny), jnp.float32), unroll=4)
+    top_send[0] = jnp.full((8, nv), jnp.max(top), jnp.float32)
+
+
+    def top_copy(axis, me, size, k, phase):
+        buf = (top_x, top_y)[phase]
+        return pltpu.make_async_remote_copy(
+            src_ref=top_send.at[phase], dst_ref=buf.at[k - 1],
+            send_sem=top_send_sem.at[phase], recv_sem=top_recv_sem.at[phase],
+            device_id={axis: lax.rem(me + k, size)}, device_id_type=MESH)
+
+    def top_all(phase):
+        buf = (top_x, top_y)[phase]
+        axis, me, size = (("gx", gx, gx_n), ("gy", gy, gy_n))[phase]
+        return pltpu.make_async_remote_copy(
+            src_ref=buf, dst_ref=buf, send_sem=top_send_sem.at[phase], recv_sem=top_recv_sem.at[phase],
+            device_id={axis: lax.rem(me + 1, size)}, device_id_type=MESH)
+
+    top_copies = [
+        [top_copy("gx", gx, gx_n, k, 0) for k in range(1, gx_n)],
+        [top_copy("gy", gy, gy_n, k, 1) for k in range(1, gy_n)],
+    ]
+    for copy in top_copies[0]:
+        copy.start()
+
     diagonal = lax.broadcasted_iota(jnp.int32, (ny, ny), 0) == lax.broadcasted_iota(jnp.int32, (ny, ny), 1)
     for i in range(nx):
         for part, out in ((0, wx), (1, wy)):
             row = jnp.broadcast_to(wind[part, pl.ds(i, 1), :], (ny, ny))
             column = jnp.sum(jnp.where(diagonal, row, 0.0), axis=1, keepdims=True)
             out[i] = jnp.broadcast_to(column, (ny, nv))
-
-    low = np.float32(SPEED_LOW) + np.float32(SPEED_SPAN) * np.float32(0.5) / np.float32(nv)
-    high = np.float32(SPEED_LOW) + np.float32(SPEED_SPAN) * np.float32(nv - 0.5) / np.float32(nv)
-    wind_x, wind_y = wind[0], wind[1]
-
-    def rate_of(k, top):
-        c = jnp.broadcast_to(cos_t[pl.ds(k, 1), 0:ny], (nx, ny))
-        n = jnp.broadcast_to(sin_t[pl.ds(k, 1), 0:ny], (nx, ny))
-        for speed in (float(low), float(high)):
-            top = jnp.maximum(top, jnp.abs(speed * c + wind_x) + jnp.abs(speed * n + wind_y))
-        return top
-
-    top = lax.fori_loop(0, n_head, rate_of, jnp.zeros((nx, ny), jnp.float32), unroll=4)
-    top_send[0] = jnp.full((8, nv), jnp.max(top), jnp.float32)
 
     speeds = SPEED_LOW + SPEED_SPAN * (
         lax.broadcasted_iota(jnp.int32, (1, nv), 1).astype(jnp.float32) + 0.5) / nv
@@ -225,97 +303,62 @@
             fy6[i, j] = jnp.abs(f) * (1.0 / (6.0 * CELL_SIZE))
         return carry
 
-    load_in.wait()
-
-    def pack_y(s, i):
-        u = us.at[s]
-        for j in range(nh):
-            ysend[s, 0, i, pl.ds(3 * j, 3), :] = u[i, j, pl.ds(8, 3), :]
-            ysend[s, 1, i, pl.ds(3 * j, 3), :] = u[i, j, pl.ds(8 + ny - 3, 3), :]
-
-    def scale_in(i, carry):
-        for j in range(nh):
-            us[0, i, j, pl.ds(8, ny), :] = acc[i, j] * SCALE
-        return carry
-
-    lax.fori_loop(0, nx, scale_in, 0)
-
-    def pack_all(s):
-        def body(i, carry):
-            pack_y(s, i)
-            return carry
-        lax.fori_loop(0, nx, body, 0)
-
-    pack_all(0)
-
-    pl.semaphore_wait(barrier, gx_n - 1 + gy_n - 1 + 2)
-
-    def top_copy(axis, me, size, k, phase):
-        buf = (top_x, top_y)[phase]
-        return pltpu.make_async_remote_copy(
-            src_ref=top_send.at[phase], dst_ref=buf.at[k - 1],
-            send_sem=top_send_sem.at[phase, k - 1], recv_sem=top_recv_sem.at[phase, k - 1],
-            device_id={axis: lax.rem(me + k, size)}, device_id_type=MESH)
-
-    top_copies = [
-        [top_copy("gx", gx, gx_n, k, 0) for k in range(1, gx_n)],
-        [top_copy("gy", gy, gy_n, k, 1) for k in range(1, gy_n)],
-    ]
-    for copy in top_copies[0]:
-        copy.start()
-    for h in range(halves):
-        start_half(0, h)
     lax.fori_loop(0, nh, flow_of, 0)
+    step_buf[...] = jnp.ones_like(step_buf)
 
     def v_pass(s):
         u = us.at[s]
         eps = eps_of(d_speed)
         e2 = eps * eps
         factor = ACCEL_MAX / (6.0 * d_speed)
-        blocks = [(i, h) for i in range(nx) for h in range(halves)]
-        shape = (nh, 8, nv)
+        blocks = [(i, h, g) for i in range(nx) for h in range(halves) for g in range(nh // V_ROWS)]
+        shape = (V_ROWS, 8, nv)
         lane = lax.broadcasted_iota(jnp.int32, (8, nv), 1)
         first = jnp.broadcast_to(lane == 0, shape)
         last = jnp.broadcast_to(lane == nv - 1, shape)
 
-        def level_0(i, h):
-            v = u[i, :, rows(h), :]
+        def level_0(i, h, g):
+            part = pl.ds(V_ROWS * g, V_ROWS)
+            v = u[i, part, rows(h), :]
             a = pltpu.roll(v, nv - 1, 2) - v
             b = v - pltpu.roll(v, 1, 2)
             q1 = jnp.where(last, b, a)
             q0 = jnp.where(first, a, b)
-            vq[i, h] = 3.0 * (q0 + q1)
-            vd[i, h] = q1 - q0
-
-        def level_1(i, h):
-            d = vd[i, h]
+            vq[i, h, part] = 3.0 * (q0 + q1)
+            vd[i, h, part] = q1 - q0
+
+        def level_1(i, h, g):
+            part = pl.ds(V_ROWS * g, V_ROWS)
+            d = vd[i, h, part]
             dm = pltpu.roll(d, 1, 2)
             s = d - dm
             c = (s * s + eps) + 0.75 * (d * dm)
             r = 1.5 * s
             p = c + r * d
             m = c - r * dm
-            vs[i, h] = s
-            vc[i, h] = c * c
-            vp[i, h] = p * p
-            vm[i, h] = m * m
-
-        def level_2(i, h):
-            s = vs[i, h]
+            vs[i, h, part] = s
+            vc[i, h, part] = c * c
+            vp[i, h, part] = p * p
+            vm[i, h, part] = m * m
+
+        def level_2(i, h, g):
+            part = pl.ds(V_ROWS * g, V_ROWS)
+            s = vs[i, h, part]
             ta = s - pltpu.roll(s, 1, 2)
             tb = pltpu.roll(s, nv - 1, 2) - s
-            p = pltpu.roll(vp[i, h], 1, 2)
-            m = pltpu.roll(vm[i, h], nv - 1, 2)
-            c = vc[i, h]
+            p = pltpu.roll(vp[i, h, part], 1, 2)
+            m = pltpu.roll(vm[i, h, part], nv - 1, 2)
+            c = vc[i, h, part]
             left = one_side(jnp.where(first, e2, p), c, m, jnp.where(first, 0.0, ta), tb)
             right = one_side(jnp.where(first, e2, m), c, p, jnp.where(first, 0.0, tb), ta)
-            vl[i, h] = left + s
-            vr[i, h] = right - s
-
-        def level_3(i, h):
-            right = pltpu.roll(vr[i, h], nv - 1, 2)
-            d3 = vq[i, h]
-            acc[i, :, inner(h), :] = factor * jnp.maximum(d3 + right, vl[i, h] - d3)
+            vl[i, h, part] = left + s
+            vr[i, h, part] = right - s
+
+        def level_3(i, h, g):
+            part = pl.ds(V_ROWS * g, V_ROWS)
+            right = pltpu.roll(vr[i, h, part], nv - 1, 2)
+            d3 = vq[i, h, part]
+            acc[i, part, inner(h), :] = factor * jnp.maximum(d3 + right, vl[i, h, part] - d3)
 
         levels = (level_0, level_1, level_2, level_3)
         apart = V_APART
@@ -346,9 +389,9 @@
                 acc[i, j, inner(h), :] += factor * value
             return carry
 
-        lax.fori_loop(0, nx, body, 0)
-
-    def x_pass(s, h):
+        lax.fori_loop(0, nx, body, 0, unroll=2)
+
+    def x_pass(s, h, store):
         u = us.at[s]
 
         def body(j, carry):
@@ -366,10 +409,11 @@
                 t1 = jnp.where(ahead, t[k + 1], t[k - 1])
                 dd = d[k] - jnp.where(ahead, d[k + 1], d[k - 1])
                 fix = one_side(b1 * b1, b2 * b2, b3 * b3, t1, t[k])
-                acc[i, j, inner(h), :] += f2 * (cells[i + 4] - cells[i + 2]) + fx6[i, j, inner(h), :] * (dd + fix)
+                term = f2 * (cells[i + 4] - cells[i + 2]) + fx6[i, j, inner(h), :] * (dd + fix)
+                store(i, j, h, acc[i, j, inner(h), :] + term)
             return carry
 
-        lax.fori_loop(0, nh, body, 0)
+        lax.fori_loop(0, nh, body, 0, unroll=2)
 
     def y_term(u, i, j, h):
         eps = eps_of(CELL_SIZE)
@@ -390,45 +434,79 @@
         fix = one_side(b1 * b1, b2 * b2, b3 * b3, s2 - s1, s3 - s2)
         return f2 * (cells[4] - cells[2]) + fy6[i, j, inner(h), :] * (s2 + fix)
 
-    def y_pass(s, h):
-        u = us.at[s]
+    def add_up(i, j, h, total):
+        acc[i, j, inner(h), :] = total
+
+    def keep_rate(i, j, h, total):
+        rate_0[i, j, inner(h), :] = jnp.minimum(total, 0.0)
+
+    def y_first(h):
+        def body(i, carry):
+            for j in range(nh):
+                acc[i, j, inner(h), :] += y_term(us.at[0], i, j, h)
+            return carry
+
+        lax.fori_loop(0, nx, body, 0, unroll=2)
+
+    def pack_first(h):
+        def body(i, carry):
+            for j in range(nh):
+                if h == 0:
+                    ysend[1, 0, i, pl.ds(3 * j, 3), :] = rate_0[i, j, 0:3, :]
+                if h == halves - 1:
+                    ysend[1, 1, i, pl.ds(3 * j, 3), :] = rate_0[i, j, ny - 3:ny, :]
+            return carry
+
+        lax.fori_loop(0, nx, body, 0)
+
+    def y_second(h):
+        dt = 0.25 * step_buf[...]
+
+        def body(i, carry):
+            for j in range(nh):
+                change = jnp.minimum(acc[i, j, inner(h), :] + y_term(us.at[1], i, j, h), 0.0)
+                fresh = (0.75 * us[0, i, j, rows(h), :] + 0.25 * us[1, i, j, rows(h), :]) + dt * change
+                us[2, i, j, rows(h), :] = fresh
+                if h == 0:
+                    ysend[2, 0, i, pl.ds(3 * j, 3), :] = fresh[0:3]
+                if h == halves - 1:
+                    ysend[2, 1, i, pl.ds(3 * j, 3), :] = fresh[5:8]
+            return carry
+
+        lax.fori_loop(0, nx, body, 0, unroll=2)
+        start_half(2, h)
+        if h == 0:
+            start_y(2, 0)
+        if h == halves - 1:
+            start_y(2, 1)
+
+    def y_third(h):
         dt = step_buf[...]
-        keep = jnp.where(s == 1, 0.75, 0.0)
-        take = jnp.where(s == 1, 0.25, 1.0)
-
-        def change(i, j):
-            total = acc[i, j, inner(h), :] + y_term(u, i, j, h)
-            return u[i, j, rows(h), :] + dt * jnp.minimum(total, 0.0)
-
-        @pl.when(s < 2)
-        def _():
-            def body(i, carry):
-                fresh = [keep * us[0, i, j, rows(h), :] + take * change(i, j) for j in range(nh)]
-                for j in range(nh):
-                    us[s + 1, i, j, rows(h), :] = fresh[j]
-                    if h == 0:
-                        ysend[s + 1, 0, i, pl.ds(3 * j, 3), :] = fresh[j][0:3]
-                    if h == halves - 1:
-                        ysend[s + 1, 1, i, pl.ds(3 * j, 3), :] = fresh[j][5:8]
-                return carry
-
-            lax.fori_loop(0, nx, body, 0)
-            start_half(s + 1, h)
-
-        @pl.when(s == 2)
-        def _():
-            def body(i, carry):
-                for j in range(nh):
-                    out_ref[i, j, inner(h), :] = change(i, j) - us[0, i, j, rows(h), :]
-                return carry
-
-            lax.fori_loop(0, nx, body, 0)
+
+        def body(i, carry):
+            for j in range(nh):
+                change = jnp.minimum(acc[i, j, inner(h), :] + y_term(us.at[2], i, j, h), 0.0)
+                out_ref[i, j, inner(h), :] = (us[2, i, j, rows(h), :] - us[0, i, j, rows(h), :]) + dt * change
+            return carry
+
+        lax.fori_loop(0, nx, body, 0, unroll=2)
 
     def receive_x(s, h):
         u = us.at[s]
         down, up = x_copies(s, h)
         pl.when(above_x)(down.wait_recv)
         pl.when(below_x)(up.wait_recv)
+
+        def stepped(halo):
+            def body(k, carry):
+                dt = step_buf[...]
+                for j in range(nh):
+                    halo[1, h, k, j] = halo[0, h, k, j] + dt * halo[1, h, k, j]
+                return carry
+            lax.fori_loop(0, 3, body, 0)
+
+        pl.when(jnp.logical_and(s == 1, above_x))(lambda: stepped(xhi))
+        pl.when(jnp.logical_and(s == 1, below_x))(lambda: stepped(xlo))
 
         @pl.when(jnp.logical_not(below_x))
         def _():
@@ -454,6 +532,16 @@
         for copy in h_copies(s, h):
             copy.wait_recv()
 
+        @pl.when(s == 1)
+        def _():
+            def body(i, carry):
+                dt = step_buf[...]
+                for k in range(3):
+                    hlo[1, h, i, k] = hlo[0, h, i, k] + dt * hlo[1, h, i, k]
+                    hhi[1, h, i, k] = hhi[0, h, i, k] + dt * hhi[1, h, i, k]
+                return carry
+            lax.fori_loop(0, nx, body, 0)
+
     def receive_y(s, which):
         u = us.at[s]
         copy = y_copies(s)[which]
@@ -463,12 +551,19 @@
         def _():
             copy.wait_recv()
 
+            halo = (yhi, ylo)[which]
+            place = pl.ds((8 + ny, 5)[which], 3)
+
+            @pl.when(s == 1)
+            def _():
+                def body(i, carry):
+                    halo[1, i] = halo[0, i] + step_buf[0:1, :] * halo[1, i]
+                    return carry
+                lax.fori_loop(0, nx, body, 0)
+
             def body(i, carry):
                 for j in range(nh):
-                    if which == 0:
-                        u[i, j, pl.ds(8 + ny, 3), :] = yhi[s, i, pl.ds(3 * j, 3), :]
-                    else:
-                        u[i, j, pl.ds(5, 3), :] = ylo[s, i, pl.ds(3 * j, 3), :]
+                    u[i, j, place, :] = halo[s, i, pl.ds(3 * j, 3), :]
                 return carry
             lax.fori_loop(0, nx, body, 0)
 
@@ -489,57 +584,78 @@
                 return carry
             lax.fori_loop(0, nx, body, 0)
 
-    def stage(s, carry):
-        v_pass(s)
-
-        @pl.when(s == 0)
-        def _():
-            for copy in top_copies[0]:
-                copy.wait_recv()
-            best = top_send[0]
-            for k in range(1, gx_n):
-                best = jnp.maximum(best, top_x[k - 1])
-            top_send[1] = best
-            for copy in top_copies[1]:
-                copy.start()
-
+    def apply_step():
+        top_all(1).wait_recv()
+        best = top_send[1]
+        for k in range(1, gy_n):
+            best = jnp.maximum(best, top_y[k - 1])
+        rate = best / CELL_SIZE + (TURN_MAX / d_theta + ACCEL_MAX / d_speed)
+        dt = CFL_NUMBER / rate
+        step_buf[...] = dt
+
+        def body(i, carry):
+            fresh = [us[0, i, j, rows(h), :] + dt * rate_0[i, j, inner(h), :] for j in range(nh) for h in range(halves)]
+            for j in range(nh):
+                for h in range(halves):
+                    us[1, i, j, rows(h), :] = fresh[j * halves + h]
+            return carry
+
+        lax.fori_loop(0, nx, body, 0)
+
+    def first_stage():
+        for h in range(1, halves):
+            start_half(0, h)
+        receive_y(0, 0)
+        receive_y(0, 1)
+        for h in range(halves):
+            y_first(h)
+            receive_h(0, h)
+            h_pass(0, h)
+            receive_x(0, h)
+            x_pass(0, h, keep_rate)
+            pack_first(h)
+            start_half(1, h)
+            if h == 0:
+                start_y(1, 0)
+                top_all(0).wait_recv()
+                best = top_send[0]
+                for k in range(1, gx_n):
+                    best = jnp.maximum(best, top_x[k - 1])
+                top_send[1] = best
+                for copy in top_copies[1]:
+                    copy.start()
+            if h == halves - 1:
+                start_y(1, 1)
+
+    def later_stage(s):
         for h in range(halves):
             receive_h(s, h)
             h_pass(s, h)
             receive_x(s, h)
-            x_pass(s, h)
+            x_pass(s, h, add_up)
             if h == 0:
                 receive_y(s, 1)
-
-                @pl.when(s == 0)
-                def _():
-                    for copy in top_copies[1]:
-                        copy.wait_recv()
-                    best = top_send[1]
-                    for k in range(1, gy_n):
-                        best = jnp.maximum(best, top_y[k - 1])
-                    rate = best / CELL_SIZE + (TURN_MAX / d_theta + ACCEL_MAX / d_speed)
-                    step_buf[...] = CFL_NUMBER / rate
-
             if h == halves - 1:
                 receive_y(s, 0)
-            y_pass(s, h)
+            pl.when(s == 1)(lambda: y_second(h))
+            pl.when(s == 2)(lambda: y_third(h))
+
+    def stage(s, carry):
+        pl.when(s == 1)(apply_step)
+        v_pass(s)
+        pl.when(s == 0)(first_stage)
+        pl.when(s > 0)(lambda: later_stage(s))
         return carry
 
     lax.fori_loop(0, 3, stage, 0)
 
-    for copy in top_copies[0] + top_copies[1]:
-        copy.wait_send()
-    for s in range(3):
-        for h in range(halves):
-            down, up = x_copies(s, h)
-            pl.when(below_x)(down.wait_send)
-            pl.when(above_x)(up.wait_send)
-            for copy in h_copies(s, h):
-                copy.wait_send()
-        down, up = y_copies(s)
-        pl.when(below_y)(down.wait_send)
-        pl.when(above_y)(up.wait_send)
+    top_all(0).wait_send()
+    top_all(1).wait_send()
+    for h in range(halves):
+        x_sent(2, h)
+        h_sent(2, h)
+    y_sent(2, 0)
+    y_sent(2, 1)
 
 
 def solution(mesh):
@@ -566,6 +682,7 @@
             scratch_shapes=[
                 pltpu.VMEM((2, nx, ny), f32),
                 pltpu.VMEM((3, nx, nh, ny + 16, nv), f32),
+                plain,
                 plain, plain, plain, plain, plain,
                 pltpu.VMEM((3, halves, 3, nh, 8, nv), f32),
                 pltpu.VMEM((3, halves, 3, nh, 8, nv), f32),
@@ -584,10 +701,10 @@
                 pltpu.VMEM((gy_n - 1, 8, nv), f32),
                 pltpu.VMEM((2, 8, nv), f32),
                 dma((2,)),
-                dma((3, halves, 2)), dma((3, halves, 2)),
-                dma((3, halves, 2)), dma((3, halves, 2)),
-                dma((3, 2)), dma((3, 2)),
-                dma((2, max(gx_n, gy_n))), dma((2, max(gx_n, gy_n))),
+                dma((halves, 2)), dma((2, halves, 2)),
+                dma((halves, 2)), dma((2, halves, 2)),
+                dma((2,)), dma((2, 2)),
+                dma((2,)), dma((2,)),
             ],
             compiler_params=pltpu.CompilerParams(
                 collective_id=0, has_side_effects=True, vmem_limit_bytes=VMEM_LIMIT),

time: 34.8 us -> 32.7 us (0.940)
  Pallas kernels: 33.8 us -> 31.7 us
    pallas_call x1, Pallas kernels: 33.8 us -> 31.7 us  [body(): pl.pallas_call(functools.partial(kernel, (gx_n, gy_n, ha_n, nx, nh, ny, n...]
where the time goes in v3:
time: 32.7 us; the launch traced here: 32.6 us
  Pallas kernels  31.7 us (97%)
  other arithmetic  0.9 us (3%)
    pallas_call x1, Pallas kernels, body(): pl.pallas_call(functools.partial(kernel, (gx_n, gy_n, ha_n, nx, nh, ny, n...  31.7 us
    transpose x1, other arithmetic, body(): return jnp.transpose(out * (2.0 / 3.0 / SCALE), (0, 2, 1, 3))  0.9 us

profile of v3, /device:TPU:1, one launch (start us, length us, event | category | flops | bytes accessed | tf_op | source)
XLA Modules:
  0.0 32.6 jit_solution(4617125552329258041)
XLA Ops:
  0.0 31.7 %shard_map.28 = f32[8,10,16,128]{3,2,1,0:T(8,128)S(1)} custom-call(f32[8,10,16,128]{3,2,1,0:T(8,128)} %bitcast.3, f32[2,8,16]{2,1,0:T(8,128)} %wind_hbm.1), custom_call_target="tpu_custom_call" | custom-call | tf_op jit(solution)/shard_map/pallas_call | solution.py:674
  31.8 0.9 %multiply_bitcast_fusion = f32[8,16,10,128]{3,1,2,0:T(8,128)} fusion(f32[8,10,16,128]{3,2,1,0:T(8,128)S(1)} %shard_map.28), kind=kLoop, calls=%fused_computation | loop fusion | flops 163840 | bytes 1310720 | tf_op jit(solution)/shard_map/transpose | solution.py:712

commit v4 on v3

--- a/solution.py
+++ b/solution.py
@@ -161,16 +161,17 @@
             device_id={"gx": gx + 1}, device_id_type=MESH)
         return down, up
 
-    def h_copies(s, h, u=None, start=8):
+    def h_copies(s, h, g, u=None, start=8):
         u = us.at[0] if u is None else u
         place = pl.ds(start + 8 * h, 8)
+        layers = pl.ds(g * (nx // 2), nx // 2)
         down = pltpu.make_async_remote_copy(
-            src_ref=u.at[:, pl.ds(0, 3), place, :], dst_ref=hhi.at[s, h],
-            send_sem=h_send.at[h, 0], recv_sem=h_recv.at[parity(s), h, 0],
+            src_ref=u.at[layers, pl.ds(0, 3), place, :], dst_ref=hhi.at[s, h, layers],
+            send_sem=h_send.at[h, g, 0], recv_sem=h_recv.at[parity(s), h, g, 0],
             device_id={"ha": h_down}, device_id_type=MESH)
         up = pltpu.make_async_remote_copy(
-            src_ref=u.at[:, pl.ds(nh - 3, 3), place, :], dst_ref=hlo.at[s, h],
-            send_sem=h_send.at[h, 1], recv_sem=h_recv.at[parity(s), h, 1],
+            src_ref=u.at[layers, pl.ds(nh - 3, 3), place, :], dst_ref=hlo.at[s, h, layers],
+            send_sem=h_send.at[h, g, 1], recv_sem=h_recv.at[parity(s), h, g, 1],
             device_id={"ha": h_up}, device_id_type=MESH)
         return down, up
 
@@ -191,8 +192,9 @@
         pl.when(above_x)(up.wait_send)
 
     def h_sent(s, h):
-        for copy in h_copies(s, h, field(s), base(s)):
-            copy.wait_send()
+        for g in range(2):
+            for copy in h_copies(s, h, g, field(s), base(s)):
+                copy.wait_send()
 
     def y_sent(s, which):
         pl.when((below_y, above_y)[which])(y_copies(s)[which].wait_send)
@@ -201,11 +203,12 @@
         if s > 0:
             x_sent(s - 1, h)
             h_sent(s - 1, h)
+        for g in range(2):
+            for copy in h_copies(s, h, g, field(s), base(s)):
+                copy.start()
         down, up = x_copies(s, h, field(s), base(s))
         pl.when(below_x)(down.start)
         pl.when(above_x)(up.start)
-        for copy in h_copies(s, h, field(s), base(s)):
-            copy.start()
 
     def start_y(s, which):
         if s > 0:
@@ -215,34 +218,6 @@
     angles = lax.broadcasted_iota(jnp.int32, (n_head, nv), 0).astype(jnp.float32) * d_theta
     cos_t[...] = jnp.cos(angles)
     sin_t[...] = jnp.sin(angles)
-
-    load_in.wait()
-
-    def pack_y(s, i):
-        u = us.at[s]
-        for j in range(nh):
-            ysend[s, 0, i, pl.ds(3 * j, 3), :] = u[i, j, pl.ds(8, 3), :]
-            ysend[s, 1, i, pl.ds(3 * j, 3), :] = u[i, j, pl.ds(8 + ny - 3, 3), :]
-
-    def scale_in(i, carry):
-        for j in range(nh):
-            us[0, i, j, pl.ds(8, ny), :] = acc[i, j] * SCALE
-        return carry
-
-    lax.fori_loop(0, nx, scale_in, 0)
-
-    def pack_all(s):
-        def body(i, carry):
-            pack_y(s, i)
-            return carry
-        lax.fori_loop(0, nx, body, 0)
-
-    pack_all(0)
-
-    pl.semaphore_wait(barrier, gx_n - 1 + gy_n - 1 + 2)
-    start_half(0, 0)
-    start_y(0, 0)
-    start_y(0, 1)
 
     low = np.float32(SPEED_LOW) + np.float32(SPEED_SPAN) * np.float32(0.5) / np.float32(nv)
     high = np.float32(SPEED_LOW) + np.float32(SPEED_SPAN) * np.float32(nv - 0.5) / np.float32(nv)
@@ -278,8 +253,36 @@
         [top_copy("gx", gx, gx_n, k, 0) for k in range(1, gx_n)],
         [top_copy("gy", gy, gy_n, k, 1) for k in range(1, gy_n)],
     ]
+    load_in.wait()
+
+    def pack_y(s, i):
+        u = us.at[s]
+        for j in range(nh):
+            ysend[s, 0, i, pl.ds(3 * j, 3), :] = u[i, j, pl.ds(8, 3), :]
+            ysend[s, 1, i, pl.ds(3 * j, 3), :] = u[i, j, pl.ds(8 + ny - 3, 3), :]
+
+    def scale_in(i, carry):
+        for j in range(nh):
+            us[0, i, j, pl.ds(8, ny), :] = acc[i, j] * SCALE
+        return carry
+
+    lax.fori_loop(0, nx, scale_in, 0)
+
+    def pack_all(s):
+        def body(i, carry):
+            pack_y(s, i)
+            return carry
+        lax.fori_loop(0, nx, body, 0)
+
+    pack_all(0)
+
+    pl.semaphore_wait(barrier, gx_n - 1 + gy_n - 1 + 2)
     for copy in top_copies[0]:
         copy.start()
+    start_half(0, 0)
+    start_y(0, 0)
+    start_y(0, 1)
+
 
     diagonal = lax.broadcasted_iota(jnp.int32, (ny, ny), 0) == lax.broadcasted_iota(jnp.int32, (ny, ny), 1)
     for i in range(nx):
@@ -368,7 +371,7 @@
                 if 0 <= k < len(blocks):
                     levels[n](*blocks[k])
 
-    def h_pass(s, h):
+    def h_pass(s, h, g):
         u = us.at[s]
         factor = TURN_MAX / (6.0 * d_theta)
 
@@ -389,7 +392,7 @@
                 acc[i, j, inner(h), :] += factor * value
             return carry
 
-        lax.fori_loop(0, nx, body, 0, unroll=2)
+        lax.fori_loop(g * (nx // 2), (g + 1) * (nx // 2), body, 0, unroll=2)
 
     def x_pass(s, h, store):
         u = us.at[s]
@@ -528,8 +531,8 @@
                 return carry
             lax.fori_loop(0, nh, body, 0)
 
-    def receive_h(s, h):
-        for copy in h_copies(s, h):
+    def receive_h(s, h, g):
+        for copy in h_copies(s, h, g):
             copy.wait_recv()
 
         @pl.when(s == 1)
@@ -540,7 +543,7 @@
                     hlo[1, h, i, k] = hlo[0, h, i, k] + dt * hlo[1, h, i, k]
                     hhi[1, h, i, k] = hhi[0, h, i, k] + dt * hhi[1, h, i, k]
                 return carry
-            lax.fori_loop(0, nx, body, 0)
+            lax.fori_loop(g * (nx // 2), (g + 1) * (nx // 2), body, 0)
 
     def receive_y(s, which):
         u = us.at[s]
@@ -607,30 +610,32 @@
             start_half(0, h)
         receive_y(0, 0)
         receive_y(0, 1)
+        top_all(0).wait_recv()
+        best = top_send[0]
+        for k in range(1, gx_n):
+            best = jnp.maximum(best, top_x[k - 1])
+        top_send[1] = best
+        for copy in top_copies[1]:
+            copy.start()
         for h in range(halves):
             y_first(h)
-            receive_h(0, h)
-            h_pass(0, h)
+            for g in range(2):
+                receive_h(0, h, g)
+                h_pass(0, h, g)
             receive_x(0, h)
             x_pass(0, h, keep_rate)
             pack_first(h)
             start_half(1, h)
             if h == 0:
                 start_y(1, 0)
-                top_all(0).wait_recv()
-                best = top_send[0]
-                for k in range(1, gx_n):
-                    best = jnp.maximum(best, top_x[k - 1])
-                top_send[1] = best
-                for copy in top_copies[1]:
-                    copy.start()
             if h == halves - 1:
                 start_y(1, 1)
 
     def later_stage(s):
         for h in range(halves):
-            receive_h(s, h)
-            h_pass(s, h)
+            for g in range(2):
+                receive_h(s, h, g)
+                h_pass(s, h, g)
             receive_x(s, h)
             x_pass(s, h, add_up)
             if h == 0:
@@ -702,7 +707,7 @@
                 pltpu.VMEM((2, 8, nv), f32),
                 dma((2,)),
                 dma((halves, 2)), dma((2, halves, 2)),
-                dma((halves, 2)), dma((2, halves, 2)),
+                dma((halves, 2, 2)), dma((2, halves, 2, 2)),
                 dma((2,)), dma((2, 2)),
                 dma((2,)), dma((2,)),
             ],

time: 32.7 us -> 30.7 us (0.939)
  Pallas kernels: 31.7 us -> 29.7 us
    pallas_call x1, Pallas kernels: 31.7 us -> 29.7 us  [body(): pl.pallas_call(functools.partial(kernel, (gx_n, gy_n, ha_n, nx, nh, ny, n...]
where the time goes in v4:
time: 30.7 us; the launch traced here: 30.6 us
  Pallas kernels  29.7 us (97%)
  other arithmetic  0.9 us (3%)
    pallas_call x1, Pallas kernels, body(): pl.pallas_call(functools.partial(kernel, (gx_n, gy_n, ha_n, nx, nh, ny, n...  29.7 us
    transpose x1, other arithmetic, body(): return jnp.transpose(out * (2.0 / 3.0 / SCALE), (0, 2, 1, 3))  0.9 us

profile of v4, /device:TPU:1, one launch (start us, length us, event | category | flops | bytes accessed | tf_op | source)
XLA Modules:
  0.0 30.6 jit_solution(3503978517127495496)
XLA Ops:
  0.0 29.7 %shard_map.28 = f32[8,10,16,128]{3,2,1,0:T(8,128)S(1)} custom-call(f32[8,10,16,128]{3,2,1,0:T(8,128)} %bitcast.3, f32[2,8,16]{2,1,0:T(8,128)} %wind_hbm.1), custom_call_target="tpu_custom_call" | custom-call | tf_op jit(solution)/shard_map/pallas_call | solution.py:679
  29.7 0.9 %multiply_bitcast_fusion = f32[8,16,10,128]{3,1,2,0:T(8,128)} fusion(f32[8,10,16,128]{3,2,1,0:T(8,128)S(1)} %shard_map.28), kind=kLoop, calls=%fused_computation | loop fusion | flops 163840 | bytes 1310720 | tf_op jit(solution)/shard_map/transpose | solution.py:717

commit v5 on v4

--- a/solution.py
+++ b/solution.py
@@ -418,11 +418,9 @@
 
         lax.fori_loop(0, nh, body, 0, unroll=2)
 
-    def y_term(u, i, j, h):
+    def y_value(cells, f2, f6):
         eps = eps_of(CELL_SIZE)
-        f2 = fy2[i, j, inner(h), :]
         ahead = f2 > 0.0
-        cells = [u[i, j, pl.ds(8 + 8 * h + r, 8), :] for r in range(-3, 4)]
         q = [cells[k + 1] - cells[k] for k in range(6)]
         d = [q[k + 1] - q[k] for k in range(5)]
         e1 = jnp.where(ahead, d[4], d[0])
@@ -435,7 +433,11 @@
         b2 = (s2 * s2 + eps) + e2k * e3
         b3 = (s3 * s3 + eps) + e3k * (e3 - s3)
         fix = one_side(b1 * b1, b2 * b2, b3 * b3, s2 - s1, s3 - s2)
-        return f2 * (cells[4] - cells[2]) + fy6[i, j, inner(h), :] * (s2 + fix)
+        return f2 * (cells[4] - cells[2]) + f6 * (s2 + fix)
+
+    def y_term(u, i, j, h):
+        cells = [u[i, j, pl.ds(8 + 8 * h + r, 8), :] for r in range(-3, 4)]
+        return y_value(cells, fy2[i, j, inner(h), :], fy6[i, j, inner(h), :])
 
     def add_up(i, j, h, total):
         acc[i, j, inner(h), :] = total
@@ -443,10 +445,29 @@
     def keep_rate(i, j, h, total):
         rate_0[i, j, inner(h), :] = jnp.minimum(total, 0.0)
 
-    def y_first(h):
+    def y_inner():
+        u = us.at[0]
+
         def body(i, carry):
             for j in range(nh):
-                acc[i, j, inner(h), :] += y_term(us.at[0], i, j, h)
+                cells = [u[i, j, pl.ds(11 + r, 8), :] for r in range(-3, 4)]
+                acc[i, j, pl.ds(3, 8), :] += y_value(cells, fy2[i, j, pl.ds(3, 8), :], fy6[i, j, pl.ds(3, 8), :])
+            return carry
+
+        lax.fori_loop(0, nx, body, 0, unroll=2)
+
+    def y_outer():
+        u = us.at[0]
+        low = lax.broadcasted_iota(jnp.int32, (8, nv), 0) < 3
+
+        def body(i, carry):
+            for j in range(nh):
+                cells = [jnp.where(low, u[i, j, pl.ds(8 + r, 8), :], u[i, j, pl.ds(16 + r, 8), :]) for r in range(-3, 4)]
+                f2 = jnp.where(low, fy2[i, j, inner(0), :], fy2[i, j, inner(1), :])
+                f6 = jnp.where(low, fy6[i, j, inner(0), :], fy6[i, j, inner(1), :])
+                value = y_value(cells, f2, f6)
+                acc[i, j, inner(0), :] += jnp.where(low, value, 0.0)
+                acc[i, j, inner(1), :] += jnp.where(low, 0.0, value)
             return carry
 
         lax.fori_loop(0, nx, body, 0, unroll=2)
@@ -476,8 +497,17 @@
                     ysend[2, 1, i, pl.ds(3 * j, 3), :] = fresh[5:8]
             return carry
 
-        lax.fori_loop(0, nx, body, 0, unroll=2)
-        start_half(2, h)
+        x_sent(1, h)
+        h_sent(1, h)
+        down, up = x_copies(2, h, field(2), base(2))
+        for g in range(2):
+            lax.fori_loop(g * (nx // 2), (g + 1) * (nx // 2), body, 0, unroll=2)
+            for copy in h_copies(2, h, g, field(2), base(2)):
+                copy.start()
+            if g == 0:
+                pl.when(below_x)(down.start)
+            else:
+                pl.when(above_x)(up.start)
         if h == 0:
             start_y(2, 0)
         if h == halves - 1:
@@ -605,11 +635,7 @@
 
         lax.fori_loop(0, nx, body, 0)
 
-    def first_stage():
-        for h in range(1, halves):
-            start_half(0, h)
-        receive_y(0, 0)
-        receive_y(0, 1)
+    def second_rates():
         top_all(0).wait_recv()
         best = top_send[0]
         for k in range(1, gx_n):
@@ -617,8 +643,16 @@
         top_send[1] = best
         for copy in top_copies[1]:
             copy.start()
+
+    def first_stage():
+        for h in range(1, halves):
+            start_half(0, h)
+        y_inner()
+        second_rates()
+        receive_y(0, 0)
+        receive_y(0, 1)
+        y_outer()
         for h in range(halves):
-            y_first(h)
             for g in range(2):
                 receive_h(0, h, g)
                 h_pass(0, h, g)

time: 30.7 us -> 30.9 us (level); the launches traced: 30.6 us -> 30.4 us
  no operation moved by 1% of the time
where the time goes in v5:
time: 30.9 us; the launch traced here: 30.4 us
  Pallas kernels  29.5 us (95%)
  other arithmetic  0.9 us (3%)
    pallas_call x1, Pallas kernels, body(): pl.pallas_call(functools.partial(kernel, (gx_n, gy_n, ha_n, nx, nh, ny, n...  29.5 us
    transpose x1, other arithmetic, body(): return jnp.transpose(out * (2.0 / 3.0 / SCALE), (0, 2, 1, 3))  0.9 us

profile of v5, /device:TPU:1, one launch (start us, length us, event | category | flops | bytes accessed | tf_op | source)
XLA Modules:
  0.0 30.4 jit_solution(5041882714735704083)
XLA Ops:
  0.0 29.5 %shard_map.28 = f32[8,10,16,128]{3,2,1,0:T(8,128)S(1)} custom-call(f32[8,10,16,128]{3,2,1,0:T(8,128)} %bitcast.3, f32[2,8,16]{2,1,0:T(8,128)} %wind_hbm.1), custom_call_target="tpu_custom_call" | custom-call | tf_op jit(solution)/shard_map/pallas_call | solution.py:713
  29.5 0.9 %multiply_bitcast_fusion = f32[8,16,10,128]{3,1,2,0:T(8,128)} fusion(f32[8,10,16,128]{3,2,1,0:T(8,128)S(1)} %shard_map.28), kind=kLoop, calls=%fused_computation | loop fusion | flops 163840 | bytes 1310720 | tf_op jit(solution)/shard_map/transpose | solution.py:751

commit v6 on v4

--- a/solution.py
+++ b/solution.py
@@ -476,8 +476,17 @@
                     ysend[2, 1, i, pl.ds(3 * j, 3), :] = fresh[5:8]
             return carry
 
-        lax.fori_loop(0, nx, body, 0, unroll=2)
-        start_half(2, h)
+        x_sent(1, h)
+        h_sent(1, h)
+        down, up = x_copies(2, h, field(2), base(2))
+        for g in range(2):
+            lax.fori_loop(g * (nx // 2), (g + 1) * (nx // 2), body, 0, unroll=2)
+            for copy in h_copies(2, h, g, field(2), base(2)):
+                copy.start()
+            if g == 0:
+                pl.when(below_x)(down.start)
+            else:
+                pl.when(above_x)(up.start)
         if h == 0:
             start_y(2, 0)
         if h == halves - 1:
@@ -608,8 +617,6 @@
     def first_stage():
         for h in range(1, halves):
             start_half(0, h)
-        receive_y(0, 0)
-        receive_y(0, 1)
         top_all(0).wait_recv()
         best = top_send[0]
         for k in range(1, gx_n):
@@ -617,6 +624,8 @@
         top_send[1] = best
         for copy in top_copies[1]:
             copy.start()
+        receive_y(0, 0)
+        receive_y(0, 1)
         for h in range(halves):
             y_first(h)
             for g in range(2):

time: 30.7 us -> 30.4 us (level)
  Pallas kernels: 29.7 us -> 29.3 us
    pallas_call x1, Pallas kernels: 29.7 us -> 29.3 us  [body(): pl.pallas_call(functools.partial(kernel, (gx_n, gy_n, ha_n, nx, nh, ny, n...]
where the time goes in v6:
time: 30.4 us; the launch traced here: 30.2 us
  Pallas kernels  29.3 us (96%)
  other arithmetic  0.9 us (3%)
    pallas_call x1, Pallas kernels, body(): pl.pallas_call(functools.partial(kernel, (gx_n, gy_n, ha_n, nx, nh, ny, n...  29.3 us
    transpose x1, other arithmetic, body(): return jnp.transpose(out * (2.0 / 3.0 / SCALE), (0, 2, 1, 3))  0.9 us

profile of v6, /device:TPU:1, one launch (start us, length us, event | category | flops | bytes accessed | tf_op | source)
XLA Modules:
  0.0 30.2 jit_solution(13075710624000646589)
XLA Ops:
  0.0 29.3 %shard_map.28 = f32[8,10,16,128]{3,2,1,0:T(8,128)S(1)} custom-call(f32[8,10,16,128]{3,2,1,0:T(8,128)} %bitcast.3, f32[2,8,16]{2,1,0:T(8,128)} %wind_hbm.1), custom_call_target="tpu_custom_call" | custom-call | tf_op jit(solution)/shard_map/pallas_call | solution.py:688
  29.3 0.9 %multiply_bitcast_fusion = f32[8,16,10,128]{3,1,2,0:T(8,128)} fusion(f32[8,10,16,128]{3,2,1,0:T(8,128)S(1)} %shard_map.28), kind=kLoop, calls=%fused_computation | loop fusion | flops 163840 | bytes 1310720 | tf_op jit(solution)/shard_map/transpose | solution.py:726
